TPU v7x, 128 devices: a whole 4x4x4 slice. The times are simulated.
128 devices in a mesh: gx: 8 (over x, core), yz: 16 (over z, y).
Axes of the slice: x: 4, y: 4, z: 4, core: 2. Of those that a mesh axis runs over, the one named last changes fastest.
Arguments:
- pressure: bfloat16 [32768, 4096], P(('gx', 'yz')), may hold values from -6 to 6
- face_block: int32 [524288], P(('gx', 'yz')), may hold values from 0 to 255
- stencil_local: int32 [32, 524288], P(None, ('gx', 'yz')), may hold values from 0 to 4095
- stencil_weight: float32 [32, 524288], P(None, ('gx', 'yz')), may hold values from 0 to 0.25
- area_normal: float32 [12, 524288], P(None, ('gx', 'yz')), may hold values from -6 to 6
- face_part: int32 [524288, 1], P(('gx', 'yz')), may hold values from 0 to 127; in each aligned block of 4096 rows (0 to 4095, 4096 to 8191, ...) at most 64 rows name the same one
- face_nodes: int32 [8, 524288], P(None, ('gx', 'yz')), may hold values from 0 to 1023
- stiffness: float32 [60, 60, 32768], P(None, None, ('gx', 'yz')), may hold values from -0.075 to 6, as said below
- connect: int32 [20, 32768], P(None, ('gx', 'yz')), may hold values from 0 to 1279
- halo_nodes: int32 [2, 16384], P(None, ('gx', 'yz')), may hold values from 0 to 1023
- node_mass: float32 [131072], P(('gx', 'yz')), may hold values from 24 to 160
- displacement: float32 [3, 131072], P(None, ('gx', 'yz')), may hold values from -6 to 6
- velocity: float32 [3, 131072], P(None, ('gx', 'yz')), may hold values from -3 to 3
Outputs:
- node_disp: float32 [3, 131072], P(None, ('gx', 'yz'))
- face_disp: float32 [12, 524288], P(None, ('gx', 'yz'))
Inputs may be any that keep to these rules, and one draw needn't show every extreme that they name: `face_part`: the faces of one device name no partition more than 64 times; in every draw some device names some partition exactly 64 times. `connect`: local node l of a partition: l < 1024 is owned, 1024 + g is entry g of the previous partition's row 1, 1152 + g entry g of the next partition's row 0 (along gx+yz). `halo_nodes`: each partition's 128 entries of row 0 are owned nodes held as ghosts by the previous partition, row 1 by the next; entries may repeat. `stiffness`: each element's matrix is symmetric positive definite.
All inputs are finite; a program needn't handle non-finite values.
Results may differ from a plain program's by a relative error of at most 0.0003.
Values sent between devices are 32-bit elements; how exact they have to be, the bound alone decides.
A program may use at most 256 MiB of HBM per device.

v0:
```python
import functools
import math

import jax
import jax.numpy as jnp
import numpy as np
from jax import lax
from jax.experimental import pallas as pl
from jax.experimental.pallas import tpu as pltpu
from jax.sharding import PartitionSpec as P

MESH = pl.DeviceIdType.MESH
F32 = jnp.float32
BF16 = jnp.bfloat16
SUBSTEPS = 4

def half_lanes(left, right):
    lane = lax.broadcasted_iota(jnp.int32, (8, 128), 1)
    return jnp.where(lane < 64, F32(left), F32(right))

def mix_weights(shapes):
    pick = lambda q, a: float(shapes[q, a])
    out = []
    for j in range(4):
        e, o = 2 * j, 2 * j + 1
        out.append((
            half_lanes(pick(0, e), pick(1, o)), half_lanes(pick(1, e), pick(0, o)),
            half_lanes(pick(2, e), pick(3, o)), half_lanes(pick(3, e), pick(2, o))))
    return out

def solid_kernel(nx, ny, shapes, s_ref, k_hbm, con_ref, halo_ref, mass_ref, disp_ref, vel_ref,
                 nd_ref, ret_ref,
                 recv, outb, kmat, ids, con_lo, con_hi, u_s, fh_s, fl_s, v_s, oh_e, oh_h, oh_x, v_x,
                 dsend, drecv, fsend, frecv,
                 k_sem, fs_sem, fr_sem, rs_sem, rr_sem, ds_sem, dr_sem, gs_sem, gr_sem):
    n = nx * ny
    gx = lax.axis_index("gx")
    yz = lax.axis_index("yz")
    me = gx * ny + yz
    dev = lambda t: (t // ny, lax.rem(t, ny))
    nxt = lax.rem(me + 1, n)
    prv = lax.rem(me + n - 1, n)
    kcopy = pltpu.make_async_copy(k_hbm, kmat, k_sem)
    kcopy.start()
    barrier = pltpu.get_barrier_semaphore()

    def greet(i, _):
        pl.semaphore_signal(barrier, inc=1, device_id=dev(lax.rem(me + i, n)), device_id_type=MESH)
        return 0
    lax.fori_loop(1, n, greet, 0)

    sub8 = lax.broadcasted_iota(jnp.int32, (8, 128), 0)
    sub128 = lax.broadcasted_iota(jnp.int32, (128, 128), 0)
    weights = mix_weights(shapes)

    con_lo[...] = con_ref[...] & 127
    con_hi[...] = con_ref[...] >> 7
    for a in range(20):
        for e in range(2):
            row = jnp.broadcast_to(con_lo[a:a + 1, 128 * e:128 * e + 128], (128, 128))
            oh_e[a * 256 + 128 * e:a * 256 + 128 * e + 128, :] = jnp.where(row == sub128, F32(1), F32(0)).T.astype(BF16)
    halo_lo = [jnp.broadcast_to(halo_ref[r:r + 1, :] & 127, (8, 128)) for r in range(2)]
    halo_hi = [jnp.broadcast_to(halo_ref[r:r + 1, :] >> 7, (8, 128)) for r in range(2)]
    for r in range(2):
        row = jnp.broadcast_to(halo_ref[r:r + 1, :] & 127, (128, 128))
        oh_h[128 * r:128 * r + 128, :] = jnp.where(row == sub128, F32(1), F32(0)).T.astype(BF16)
    stack = lambda ref, c: jnp.concatenate([ref[c:c + 1, 128 * h:128 * h + 128] for h in range(8)], axis=0)
    disp = [stack(disp_ref, c) for c in range(3)]
    vel = [stack(vel_ref, c) for c in range(3)]
    mass = stack(mass_ref, 0)

    pl.semaphore_wait(barrier, n - 1)

    def near(src, dst, ss, rs, t):
        return pltpu.make_async_remote_copy(src_ref=src, dst_ref=dst, send_sem=ss, recv_sem=rs, device_id=dev(t), device_id_type=MESH)

    def disp_copies(step):
        return [near(dsend.at[step, 1], drecv.at[step, 0], ds_sem.at[step, 1], dr_sem.at[step, 0], nxt),
                near(dsend.at[step, 0], drecv.at[step, 1], ds_sem.at[step, 0], dr_sem.at[step, 1], prv)]

    def force_copies(step):
        return [near(fsend.at[step, 0], frecv.at[step, 1], gs_sem.at[step, 0], gr_sem.at[step, 1], prv),
                near(fsend.at[step, 1], frecv.at[step, 0], gs_sem.at[step, 1], gr_sem.at[step, 0], nxt)]

    def send_disp(step, disp):
        for r in range(2):
            for c in range(3):
                g = jnp.where(halo_hi[r] == sub8, lane_take(disp[c], halo_lo[r]), F32(0))
                dsend[step, r, c:c + 1, :] = jnp.sum(g, axis=0, keepdims=True)
        for cp in disp_copies(step):
            cp.start()

    def internal(step, disp):
        cps = disp_copies(step)
        for cp in cps:
            cp.wait()
        ghost = [jnp.where(me > 0, drecv[step, 0, 0:3, :], F32(0)), jnp.where(me < n - 1, drecv[step, 1, 0:3, :], F32(0))]
        for c in range(3):
            rows = [disp[c][h:h + 1, :] for h in range(8)] + [ghost[0][c:c + 1, :], ghost[1][c:c + 1, :]]
            rows = [jnp.broadcast_to(r, (8, 128)) for r in rows]
            for at in range(3):
                for e in range(2):
                    lo = con_lo[8 * at:8 * at + 8, 128 * e:128 * e + 128]
                    hi = con_hi[8 * at:8 * at + 8, 128 * e:128 * e + 128]
                    acc = lane_take(rows[0], lo)
                    for h in range(1, 10):
                        acc = jnp.where(hi == h, lane_take(rows[h], lo), acc)
                    u_s[c, 8 * at:8 * at + 8, 128 * e:128 * e + 128] = acc

        def multiply(a, acc):
            for c in range(3):
                acc = acc + kmat[c * 20 + a] * u_s[c, pl.ds(a, 1), :]
            return acc
        force = lax.fori_loop(0, 20, multiply, jnp.zeros((60, 256), F32))
        fh = force.astype(BF16).astype(F32)
        fh_s[...] = fh
        fl_s[...] = force - fh
        sub16 = lax.broadcasted_iota(jnp.int32, (16, 256), 0)
        for a in range(20):
            mask = jnp.broadcast_to(con_hi[a:a + 1, :], (16, 256)) == sub16
            for c in range(3):
                for k, part in enumerate((fh_s, fl_s)):
                    row = jnp.broadcast_to(part[20 * c + a:20 * c + a + 1, :], (16, 256))
                    v_s[48 * k + 16 * c:48 * k + 16 * c + 16, a * 256:a * 256 + 256] = jnp.where(mask, row, F32(0)).astype(BF16)
        both = jnp.dot(v_s[...], oh_e[...], preferred_element_type=F32)
        total = both[:48] + both[48:]
        for k in range(2):
            for c in range(3):
                fsend[step, k, c:c + 1, :] = total[16 * c + 8 + k:16 * c + 9 + k, :]
        for cp in force_copies(step):
            cp.start()
        return [total[16 * c:16 * c + 8, :] for c in range(3)]

    def advance(step, own, ext, disp, vel):
        for cp in force_copies(step):
            cp.wait()
        got = [jnp.where(me > 0, frecv[step, 0, 0:3, :], F32(0)), jnp.where(me < n - 1, frecv[step, 1, 0:3, :], F32(0))]
        parts = []
        for c in range(3):
            cols = []
            for r in range(2):
                x = jnp.where(halo_hi[r] == sub8, jnp.broadcast_to(got[r][c:c + 1, :], (8, 128)), F32(0))
                cols.append(x)
            parts.append(jnp.concatenate(cols, axis=1))
        x = jnp.concatenate(parts, axis=0)
        xh = x.astype(BF16).astype(F32)
        lhs = jnp.concatenate([xh, x - xh], axis=0).astype(BF16)
        both = jnp.dot(lhs, oh_h[...], preferred_element_type=F32)
        add = both[:24] + both[24:]
        vel = [vel[c] + (ext[c] - (own[c] + add[8 * c:8 * c + 8, :])) / mass for c in range(3)]
        disp = [disp[c] + vel[c] for c in range(3)]
        return disp, vel

    send_disp(0, disp)

    def fwd(i):
        t = lax.rem(me + i, n)
        return near(s_ref.at[t], recv.at[me], fs_sem.at[i], fr_sem.at[i], t)

    def fwd_start(i, _):
        fwd(i).start()
        return 0
    lax.fori_loop(1, n, fwd_start, 0)
    recv[me] = s_ref[me]
    kcopy.wait()
    own = internal(0, disp)

    def fwd_wait(i, _):
        fwd(i).wait()
        return 0
    lax.fori_loop(1, n, fwd_wait, 0)

    sub128h = lax.broadcasted_iota(jnp.int32, (128, 128), 0).astype(jnp.int16)

    def gather_load(t, acc):
        base = pl.multiple_of(t * 8, 8)
        get = lambda r: recv[pl.ds(base, 8), r, :]
        loads = []
        for c in range(3):
            t0, t1 = get(2 * c), get(2 * c + 1)
            r0, r1 = pltpu.roll(t0, 64, 1), pltpu.roll(t1, 64, 1)
            loads.append([weights[j][0] * t0 + weights[j][1] * r0 + weights[j][2] * t1 + weights[j][3] * r1 for j in range(4)])
        for j in range(4):
            idx = get(6 + j).astype(jnp.int32)
            ids[j, pl.ds(base, 8), :] = idx
            lo, hi = idx & 127, idx >> 7
            highs = [loads[c][j].astype(BF16).astype(F32) for c in range(3)]
            lows = [loads[c][j] - highs[c] for c in range(3)]
            for s in range(8):
                at = (j * 8 + s) * 128
                row = jnp.broadcast_to(lo[s:s + 1, :], (128, 128)).astype(jnp.int16)
                oh_x[:, at:at + 128] = jnp.where(row == sub128h, BF16(1), BF16(0))
                mask = jnp.broadcast_to(hi[s:s + 1, :], (8, 128)) == sub8
                v_x[:, at:at + 128] = jnp.concatenate(
                    [jnp.where(mask, jnp.broadcast_to(p[s:s + 1, :], (8, 128)), F32(0)) for p in highs + lows], axis=0).astype(BF16)
        return acc + lax.dot_general(v_x[...], oh_x[...], (((1,), (1,)), ((), ())), preferred_element_type=F32)
    both = lax.fori_loop(0, n // 8, gather_load, jnp.zeros((48, 128), F32))
    ext = [both[8 * c:8 * c + 8] + both[24 + 8 * c:32 + 8 * c] for c in range(3)]

    disp, vel = advance(0, own, ext, disp, vel)
    for step in range(1, SUBSTEPS):
        send_disp(step, disp)
        own = internal(step, disp)
        disp, vel = advance(step, own, ext, disp, vel)
    for c in range(3):
        for h in range(8):
            nd_ref[c:c + 1, 128 * h:128 * h + 128] = disp[c][h:h + 1, :]
            u_s[c, h:h + 1, 0:128] = disp[c][h:h + 1, :]

    def back(t):
        base = pl.multiple_of(t * 8, 8)
        idx = [ids[j, pl.ds(base, 8), :] for j in range(4)]
        for c in range(3):
            p0 = p1 = q0 = q1 = jnp.zeros((8, 128), F32)
            for j in range(4):
                lo, hi = idx[j] & 127, idx[j] >> 7
                acc = lane_take(jnp.broadcast_to(u_s[c, 0:1, 0:128], (8, 128)), lo)
                for h in range(1, 8):
                    acc = jnp.where(hi == h, lane_take(jnp.broadcast_to(u_s[c, h:h + 1, 0:128], (8, 128)), lo), acc)
                p0 = p0 + weights[j][0] * acc
                q0 = q0 + weights[j][1] * acc
                p1 = p1 + weights[j][2] * acc
                q1 = q1 + weights[j][3] * acc
            outb[pl.ds(base, 8), 2 * c, :] = p0 + pltpu.roll(q0, 64, 1)
            outb[pl.ds(base, 8), 2 * c + 1, :] = p1 + pltpu.roll(q1, 64, 1)

    def back_loop(t, _):
        back(t)
        return 0
    lax.fori_loop(0, n // 8, back_loop, 0)

    def ret(i):
        t = lax.rem(me + i, n)
        return near(outb.at[t], ret_ref.at[me], rs_sem.at[i], rr_sem.at[i], t)

    def ret_start(i, _):
        ret(i).start()
        return 0
    lax.fori_loop(1, n, ret_start, 0)
    ret_ref[me] = outb[me]

    def ret_wait(i, _):
        ret(i).wait()
        return 0
    lax.fori_loop(1, n, ret_wait, 0)


def solid(send, stiffness, connect, halo, mass, disp, vel, nx, ny, shapes):
    n = nx * ny
    V = pl.BlockSpec(memory_space=pltpu.VMEM)
    A = pl.BlockSpec(memory_space=pl.ANY)
    D = pltpu.SemaphoreType.DMA
    connect = jnp.pad(connect, ((0, 4), (0, 0)))
    return pl.pallas_call(
        functools.partial(solid_kernel, nx, ny, shapes),
        out_shape=(jax.ShapeDtypeStruct(disp.shape, F32), jax.ShapeDtypeStruct((n, 6, 128), F32)),
        in_specs=[V, A, V, V, V, V, V],
        out_specs=(V, V),
        scratch_shapes=[
            pltpu.VMEM((n, 10, 128), F32), pltpu.VMEM((n, 6, 128), F32), pltpu.VMEM((60, 60, 256), F32),
            pltpu.VMEM((4, n, 128), jnp.int32), pltpu.VMEM((24, 256), jnp.int32), pltpu.VMEM((24, 256), jnp.int32),
            pltpu.VMEM((3, 24, 256), F32), pltpu.VMEM((60, 256), F32), pltpu.VMEM((60, 256), F32),
            pltpu.VMEM((96, 5120), BF16), pltpu.VMEM((5120, 128), BF16), pltpu.VMEM((256, 128), BF16),
            pltpu.VMEM((128, 4096), BF16), pltpu.VMEM((48, 4096), BF16),
            pltpu.VMEM((SUBSTEPS, 2, 8, 128), F32), pltpu.VMEM((SUBSTEPS, 2, 8, 128), F32),
            pltpu.VMEM((SUBSTEPS, 2, 8, 128), F32), pltpu.VMEM((SUBSTEPS, 2, 8, 128), F32),
            D, D((n,)), D((n,)), D((n,)), D((n,)), D((SUBSTEPS, 2)), D((SUBSTEPS, 2)), D((SUBSTEPS, 2)), D((SUBSTEPS, 2))],
        compiler_params=pltpu.CompilerParams(collective_id=0, has_side_effects=True, vmem_limit_bytes=48 * 2**20),
        name="solid",
    )(send, stiffness, connect, halo, mass.reshape(1, -1), disp, vel)


STRIDE = 40
UNR = 32
TAKE = lax.GatherDimensionNumbers(
    offset_dims=(), collapsed_slice_dims=(1,), start_index_map=(1,), operand_batching_dims=(0,), start_indices_batching_dims=(0,)
)

def lane_take(x, idx):
    return lax.gather(x, idx[..., None], TAKE, slice_sizes=(1, 1), mode=lax.GatherScatterMode.PROMISE_IN_BOUNDS)

def stencil_kernel(fb_ref, pr_ref, loc_ref, w_ref, an_ref, out_ref, tab32, tab, idxt, wt, res):
    def relayout(b, _):
        r0 = pl.multiple_of(b * 16, 16)
        for t in range(32):
            x = pr_ref[pl.ds(r0, 16), 128 * t:128 * t + 128].astype(jnp.float32)
            tab32[pl.ds(t, 8, stride=STRIDE), :] = x[:8]
            tab32[pl.ds(8 * STRIDE + t, 8, stride=STRIDE), :] = x[8:]
        for n in range(16):
            tab[pl.ds(pl.multiple_of((r0 + n) * 32, 32), 32), :] = tab32[n * STRIDE:n * STRIDE + 32, :].astype(jnp.bfloat16)
        return 0
    lax.fori_loop(0, 16, relayout, 0)
    for i in range(8):
        idxt[128 * i:128 * i + 128, :] = jnp.concatenate(
            [loc_ref[:, a * 1024 + 128 * i:a * 1024 + 128 * i + 128] for a in range(4)], axis=0).T
        wt[128 * i:128 * i + 128, :] = jnp.concatenate(
            [w_ref[:, a * 1024 + 128 * i:a * 1024 + 128 * i + 128] for a in range(4)], axis=0).T
    lane = lax.broadcasted_iota(jnp.int32, (16, 128), 1)
    sub = lax.broadcasted_iota(jnp.int32, (16, 128), 0).astype(jnp.int16)
    grp = (lane // 32).astype(jnp.int16)
    m_lo = grp < 2
    m0 = grp == 0
    m2 = grp == 2

    def main(gg, _):
        for uu in range(UNR // 8):
            base = pl.multiple_of(gg * UNR + 8 * uu, 8)
            rows = []
            for u in range(8):
                g = base + u
                row = jnp.broadcast_to(idxt[pl.ds(g, 1), :], (16, 128))
                lo = (row & 127).astype(jnp.int16)
                hi = (row >> 7).astype(jnp.int16)
                cl = hi < 16
                mine = (hi & 15) == sub
                xs = []
                for a in range(4):
                    off = pl.multiple_of(fb_ref[a * 1024 + g] * 32, 32)
                    xs.append(jnp.where(cl, lane_take(tab[pl.ds(off, 16), :], lo), lane_take(tab[pl.ds(off + 16, 16), :], lo)))
                x = jnp.where(m_lo, jnp.where(m0, xs[0], xs[1]), jnp.where(m2, xs[2], xs[3]))
                x = jnp.where(mine, x, jnp.bfloat16(0)).astype(jnp.float32)
                rows.append(jnp.sum(x[:8] + x[8:], axis=0, keepdims=True))
            res[pl.ds(base, 8), :] = jnp.concatenate(rows, axis=0) * wt[pl.ds(base, 8), :]
        return 0
    lax.fori_loop(0, 1024 // UNR, main, 0)
    for i in range(8):
        rt = res[128 * i:128 * i + 128, :].T
        for a in range(4):
            f0 = a * 1024 + 128 * i
            fp = jnp.concatenate([jnp.sum(rt[a * 32 + 8 * q:a * 32 + 8 * q + 8], axis=0, keepdims=True) for q in range(4)], axis=0)
            fp3 = jnp.concatenate([fp, fp, fp], axis=0)
            out_ref[:, f0:f0 + 128] = -(an_ref[:, f0:f0 + 128] * fp3)

def stencil(face_block, pressure, local, weight, area):
    V = pl.BlockSpec(memory_space=pltpu.VMEM)
    return pl.pallas_call(
        stencil_kernel,
        out_shape=jax.ShapeDtypeStruct((12, 4096), jnp.float32),
        in_specs=[pl.BlockSpec(memory_space=pltpu.SMEM), V, V, V, V],
        out_specs=V,
        scratch_shapes=[pltpu.VMEM((16 * STRIDE, 128), jnp.float32), pltpu.VMEM((8192, 128), jnp.bfloat16), pltpu.VMEM((1024, 128), jnp.int32),
                        pltpu.VMEM((1024, 128), jnp.float32), pltpu.VMEM((1024, 128), jnp.float32)],
        compiler_params=pltpu.CompilerParams(vmem_limit_bytes=40 * 2**20),
        name="stencil",
    )(face_block, pressure, local, weight, area)


def shape_table():
    corner_u = [-1, 1, 1, -1, 0, 1, 0, -1]
    corner_v = [-1, -1, 1, 1, -1, 0, 1, 0]
    gauss_point = 1.0 / math.sqrt(3.0)
    points = [
        (-gauss_point, -gauss_point),
        (gauss_point, -gauss_point),
        (gauss_point, gauss_point),
        (-gauss_point, gauss_point),
    ]
    shape_values = np.zeros((4, 8), np.float32)
    for position, (coord_u, coord_v) in enumerate(points):
        for corner in range(8):
            node_u = corner_u[corner]
            node_v = corner_v[corner]
            if corner < 4:
                entry_value = (
                    0.25
                    * (1 + coord_u * node_u)
                    * (1 + coord_v * node_v)
                    * (coord_u * node_u + coord_v * node_v - 1)
                )
            elif node_u == 0:
                entry_value = 0.5 * (1 - coord_u * coord_u) * (1 + coord_v * node_v)
            else:
                entry_value = 0.5 * (1 + coord_u * node_u) * (1 - coord_v * coord_v)
            shape_values[position, corner] = entry_value
    return shape_values


def hot_pair(indices, extent):
    lanes_width = 32
    upper_count = -(-extent // lanes_width)
    upper_hot = (
        indices[None, :] // lanes_width == lax.broadcasted_iota(jnp.int32, (upper_count, 1), 0)
    ).astype(jnp.float32)
    lower_hot = (
        indices[None, :] % lanes_width == lax.broadcasted_iota(jnp.int32, (lanes_width, 1), 0)
    ).astype(jnp.float32)
    return (upper_hot, lower_hot)


def pick_cols(table, hots):
    upper_hot, lower_hot = hots
    lanes_width = lower_hot.shape[0]
    upper_count = upper_hot.shape[0]
    comps, extent = table.shape
    grid = (
        table.reshape(comps, upper_count, lanes_width)
        .transpose(1, 0, 2)
        .reshape(upper_count, comps * lanes_width)
    )
    rows_out = lax.dot_general(
        grid,
        upper_hot,
        (((0,), (0,)), ((), ())),
        precision=lax.Precision.HIGHEST,
        preferred_element_type=jnp.float32,
    )
    return jnp.sum(rows_out.reshape(comps, lanes_width, -1) * lower_hot[None], axis=1)


def spread_cols(values, hots):
    upper_hot, lower_hot = hots
    lanes_width = lower_hot.shape[0]
    upper_count = upper_hot.shape[0]
    comps = values.shape[0]
    masked = (values[:, None, :] * lower_hot[None]).reshape(comps * lanes_width, -1)
    summed = lax.dot_general(
        masked,
        upper_hot,
        (((1,), (1,)), ((), ())),
        precision=lax.Precision.HIGHEST,
        preferred_element_type=jnp.float32,
    )
    return (
        summed.reshape(comps, lanes_width, upper_count)
        .transpose(0, 2, 1)
        .reshape(comps, upper_count * lanes_width)
    )


def arrival_order(target, devices):
    row_count = target.shape[0]
    group_rows = min(512, row_count)
    groups = row_count // group_rows
    onehot = (target[:, None] == jnp.arange(devices, dtype=jnp.int32)[None, :]).astype(jnp.bfloat16)
    onehot = onehot.reshape(groups, group_rows, devices)
    lower_ones = (
        lax.broadcasted_iota(jnp.int32, (group_rows, group_rows), 0)
        > lax.broadcasted_iota(jnp.int32, (group_rows, group_rows), 1)
    ).astype(jnp.bfloat16)
    before = jnp.einsum("ij,gjd->gid", lower_ones, onehot, preferred_element_type=jnp.float32)
    onehot_float = onehot.astype(jnp.float32)
    totals = jnp.sum(onehot_float, axis=1)
    offsets = jnp.cumsum(totals, axis=0) - totals
    placed = jnp.sum((before + offsets[:, None, :]) * onehot_float, axis=2)
    return placed.reshape(row_count).astype(jnp.int32)


def shards(
    pressure,
    face_block,
    stencil_local,
    stencil_weight,
    area_normal,
    face_part,
    face_nodes,
    stiffness,
    connect,
    halo_nodes,
    node_mass,
    displacement,
    velocity,
):
    gx_size = lax.axis_size("gx")
    yz_size = lax.axis_size("yz")
    devices = gx_size * yz_size
    face_count = face_block.shape[0]
    capacity = 2 * face_count // devices
    slot_total = devices * capacity
    traction = stencil(face_block, pressure, stencil_local, stencil_weight, area_normal)
    target = face_part[:, 0]
    slots = target * capacity + arrival_order(target, devices)
    slot_hots = hot_pair(slots, slot_total)
    packed = spread_cols(
        jnp.concatenate([traction, face_nodes.astype(jnp.float32)], axis=0), slot_hots
    )
    send = packed.reshape(10, 2, devices, capacity).transpose(2, 0, 1, 3).reshape(devices, 10, 2 * capacity)
    node_disp, returned = solid(
        send, stiffness, connect, halo_nodes, node_mass, displacement, velocity, gx_size, yz_size, shape_table()
    )
    returned = returned.reshape(devices, 6, 2, capacity).transpose(1, 2, 0, 3).reshape(12, slot_total)
    face_disp = pick_cols(returned, slot_hots)
    return (node_disp, face_disp)


def solution(mesh):
    in_specs = (
        P(("gx", "yz"), None),
        P(("gx", "yz")),
        P(None, ("gx", "yz")),
        P(None, ("gx", "yz")),
        P(None, ("gx", "yz")),
        P(("gx", "yz"), None),
        P(None, ("gx", "yz")),
        P(None, None, ("gx", "yz")),
        P(None, ("gx", "yz")),
        P(None, ("gx", "yz")),
        P(("gx", "yz")),
        P(None, ("gx", "yz")),
        P(None, ("gx", "yz")),
    )
    out_specs = (P(None, ("gx", "yz")), P(None, ("gx", "yz")))
    return jax.shard_map(shards, mesh=mesh, in_specs=in_specs, out_specs=out_specs, check_vma=False)
```

profile of v0, /device:TPU:1, one launch (start us, length us, event | category | flops | bytes accessed | tf_op | source)
XLA Modules:
  0.0 126.8 jit_solution(1156528473386782825)
XLA Ops:
  0.6 0.5 broadcast.110
  1.1 1.4 %fusion.24 = (s32[4096]{0:T(1024)S(1)}, s32[4096,1]{0,1:T(1,128)S(1)}) fusion(s32[4096,1]{0,1:T(1,128)} %param.18, s32[]{:T(128)} %broadcast.110), kind=kLoop, calls=%fused_computation.33 | loop fusion | flops 4096 | bytes 49156 | tf_op args[5]
  2.6 0.3 convert_reduce_fusion
  2.9 0.0 copy-start.1
  2.9 0.0 copy-start.2
  2.9 0.0 copy-start.3
  2.9 0.0 copy-start.4
  2.9 0.0 copy-start.5
  2.9 1.0 fusion.7
  4.0 0.0 copy-start.12
  4.0 0.0 copy-start.10
  4.0 0.5 copy-done.1
  4.5 0.1 copy-done.2
  4.6 0.2 copy-done.3
  4.7 0.1 copy-done.4
  4.8 16.7 %stencil.1 = f32[12,4096]{1,0:T(8,128)S(1)} custom-call(s32[4096]{0:T(1024)S(1)} %copy-done.5, bf16[256,4096]{1,0:T(8,128)(2,1)S(1)} %copy-done.1, s32[32,4096]{1,0:T(8,128)S(1)} %copy-done.2, f32[32,4096]{1,0:T(8,128)S(1)} %copy-done.3, f32[12,4096]{1,0:T(8,128)S(1)} %copy-done.4), custom_call_target="tpu_custom_call" | custom-call | tf_op jit(solution)/shard_map/stencil/pallas_call | solution.py:336
  21.6 5.7 %fusion.12 = f32[20,256,32]{1,2,0:T(8,128)S(1)} fusion(s32[4096]{0:T(1024)S(1)} %get-tuple-element.7, f32[32,4096]{1,0:T(8,128)S(1)} %fusion.20, f32[20,4096]{1,0:T(8,128)S(1)} %pad_maximum_fusion), kind=kOutput, calls=%fused_computation.15 | convolution fusion | flops 8056733696 | bytes 1523712 | tf_op jit(solution)/shard_map/dot_general | solution.py:416
  27.3 0.9 copy.20
  28.2 1.5 %reshape_reshape.6 = f32[10,2,128,64]{3,2,1,0:T(8,128)} reshape(f32[20,256,32]{2,1,0:T(8,128)S(1)} %copy.20) | data formatting | bytes 1310720 | tf_op jit(solution)/shard_map/reshape;reshape | solution.py:476
  29.7 0.0 copy-start.9
  29.7 1.8 %copy.21 = f32[128,10,2,64]{0,3,2,1:T(8,128)S(1)} copy(f32[128,10,2,64]{3,0,2,1:T(8,128)} %bitcast.36) | data formatting | bytes 1310720 | tf_op jit(solution)/shard_map/transpose | solution.py:476
  31.5 0.5 copy.22.s_ref
  32.0 0.0 copy-start
  32.1 2.1 %copy-done = f32[60,60,256]{2,1,0:T(8,128)S(1)} copy-done((f32[60,60,256]{2,1,0:T(8,128)S(1)}, f32[60,60,256]{2,1,0:T(8,128)}, u32[]{:S(2)}) %copy-start) | copy-done | bytes 3686424
  34.2 86.5 %solid.1 = (f32[3,1024]{1,0:T(4,128)S(1)}, f32[128,6,128]{2,1,0:T(8,128)S(1)}) custom-call(f32[128,10,128]{2,1,0:T(8,128)S(1)} %copy.22.s_ref, f32[60,60,256]{2,1,0:T(8,128)S(1)} %copy-done, s32[24,256]{1,0:T(8,128)S(1)} %pad.4.con_ref, s32[2,128]{1,0:T(2,128)S(1)} %copy-done.9, f32[1,1024]{1,0:T(1,128)S(1)} %bitcast.34, f32[3,1024]{1,0:T(4,128)S(1)} %copy-done.6, ...), custom_call_target="tpu_custom_call" | custom-call | tf_op jit(solution)/shard_map/solid/pallas_call | solution.py:254
  120.6 0.2 copy.23
  120.8 0.3 copy.24
  121.1 0.3 reshape_reshape.7
  121.4 0.4 copy.25
  121.8 0.3 copy-done.11
  122.1 4.1 %multiply_reduce_fusion = f32[12,4096]{1,0:T(8,128)} fusion(f32[32,4096]{1,0:T(8,128)S(1)} %copy-done.11, s32[4096]{0:T(1024)S(1)} %get-tuple-element.7, f32[256,12,32]{0,2,1:T(8,128)S(1)} %copy.25), kind=kOutput, calls=%fused_computation.2 | convolution fusion | flops 4835983360 | bytes 1130496 | tf_op jit(solution)/shard_map/dot_general | solution.py:400
  126.2 0.6 copy.28
  (23 shorter events, 0.2 us)
Async XLA Ops:
  2.9 1.6 %copy-start.1 = (bf16[256,4096]{1,0:T(8,128)(2,1)S(1)}, bf16[256,4096]{1,0:T(8,128)(2,1)}, u32[]{:S(2)}) copy-start(bf16[256,4096]{1,0:T(8,128)(2,1)} %pr_ref.1) | copy-start | bytes 6291460
  2.9 1.7 %copy-start.2 = (s32[32,4096]{1,0:T(8,128)S(1)}, s32[32,4096]{1,0:T(8,128)}, u32[]{:S(2)}) copy-start(s32[32,4096]{1,0:T(8,128)} %loc_ref.1) | copy-start | bytes 1572868
  2.9 1.8 %copy-start.3 = (f32[32,4096]{1,0:T(8,128)S(1)}, f32[32,4096]{1,0:T(8,128)}, u32[]{:S(2)}) copy-start(f32[32,4096]{1,0:T(8,128)} %w_ref.1) | copy-start | bytes 1572868
  2.9 1.9 %copy-start.4 = (f32[12,4096]{1,0:T(8,128)S(1)}, f32[12,4096]{1,0:T(8,128)}, u32[]{:S(2)}) copy-start(f32[12,4096]{1,0:T(8,128)} %an_ref.1) | copy-start | bytes 589828
  2.9 1.9 %copy-start.5 = (s32[4096]{0:T(1024)S(1)}, s32[4096]{0:T(1024)}, u32[]{:S(2)}) copy-start(s32[4096]{0:T(1024)} %fb_ref.1) | copy-start | bytes 49156
  4.0 17.6 %copy-start.12 = (s32[8,4096]{1,0:T(8,128)S(1)}, s32[8,4096]{1,0:T(8,128)}, u32[]{:S(2)}) copy-start(s32[8,4096]{1,0:T(8,128)} %param.19) | copy-start | bytes 393220
  4.0 17.6 %copy-start.10 = (f32[32,4096]{1,0:T(8,128)}, f32[32,4096]{1,0:T(8,128)S(1)}, u32[]{:S(2)}) copy-start(f32[32,4096]{1,0:T(8,128)S(1)} %fusion.20) | copy-start | bytes 1572868
  29.7 2.3 %copy-start.13 = (s32[20,256]{1,0:T(8,128)S(1)}, s32[20,256]{1,0:T(8,128)}, u32[]{:S(2)}) copy-start(s32[20,256]{1,0:T(8,128)} %param.21) | copy-start | bytes 61444
  29.7 2.3 %copy-start.6 = (f32[3,1024]{1,0:T(4,128)S(1)}, f32[3,1024]{1,0:T(4,128)}, u32[]{:S(2)}) copy-start(f32[3,1024]{1,0:T(4,128)} %disp_ref.1) | copy-start | bytes 36868
  29.7 2.3 %copy-start.7 = (f32[3,1024]{1,0:T(4,128)S(1)}, f32[3,1024]{1,0:T(4,128)}, u32[]{:S(2)}) copy-start(f32[3,1024]{1,0:T(4,128)} %vel_ref.1) | copy-start | bytes 36868
  29.7 2.3 %copy-start.8 = (f32[1024]{0:T(1024)S(1)}, f32[1024]{0:T(1024)}, u32[]{:S(2)}) copy-start(f32[1024]{0:T(1024)} %param.23) | copy-start | bytes 12292
  29.7 2.3 %copy-start.9 = (s32[2,128]{1,0:T(2,128)S(1)}, s32[2,128]{1,0:T(2,128)}, u32[]{:S(2)}) copy-start(s32[2,128]{1,0:T(2,128)} %halo_ref.1) | copy-start | bytes 3076
  32.0 2.1 %copy-start = (f32[60,60,256]{2,1,0:T(8,128)S(1)}, f32[60,60,256]{2,1,0:T(8,128)}, u32[]{:S(2)}) copy-start(f32[60,60,256]{2,1,0:T(8,128)} %k_hbm.1) | copy-start | bytes 11059204
  121.1 1.0 copy-start.11
where the time goes:
time: 127 us
  Pallas kernels  103 us (81%)
  matrix products  10.7 us (8%)
  local copies, waits for them, and re-layouts  10.2 us (8%)
  other arithmetic  1.83 us (1%)
    pallas_call x1, Pallas kernels, solid(): pl.pallas_call(functools.partial(solid_kernel, nx, ny, shapes), out_shape...  86.5 us
    pallas_call x1, Pallas kernels, stencil(): pl.pallas_call(stencil_kernel, out_shape=jax.ShapeDtypeStruct((12, 4096),...  16.7 us
    dot_general x1, matrix products, spread_cols(): lax.dot_general(masked, upper_hot, (((1,), (1,)), ((), ())), precision=la...  5.72 us
    unnamed x31, local copies, waits for them, and re-layouts  4.36 us
    dot_general x1, matrix products, pick_cols(): lax.dot_general(grid, upper_hot, (((0,), (0,)), ((), ())), precision=lax....  4.07 us

commit v1 on v0

--- a/solution.py
+++ b/solution.py
@@ -82,18 +82,39 @@
         return [near(fsend.at[step, 0], frecv.at[step, 1], gs_sem.at[step, 0], gr_sem.at[step, 1], prv),
                 near(fsend.at[step, 1], frecv.at[step, 0], gs_sem.at[step, 1], gr_sem.at[step, 0], nxt)]
 
+    def start_both(copies):
+        up, down = copies
+
+        @pl.when(me < n - 1)
+        def _():
+            up.start()
+
+        @pl.when(me > 0)
+        def _():
+            down.start()
+
+    def wait_both(copies):
+        up, down = copies
+
+        @pl.when(me < n - 1)
+        def _():
+            up.wait_send()
+            down.wait_recv()
+
+        @pl.when(me > 0)
+        def _():
+            down.wait_send()
+            up.wait_recv()
+
     def send_disp(step, disp):
         for r in range(2):
             for c in range(3):
                 g = jnp.where(halo_hi[r] == sub8, lane_take(disp[c], halo_lo[r]), F32(0))
                 dsend[step, r, c:c + 1, :] = jnp.sum(g, axis=0, keepdims=True)
-        for cp in disp_copies(step):
-            cp.start()
+        start_both(disp_copies(step))
 
     def internal(step, disp):
-        cps = disp_copies(step)
-        for cp in cps:
-            cp.wait()
+        wait_both(disp_copies(step))
         ghost = [jnp.where(me > 0, drecv[step, 0, 0:3, :], F32(0)), jnp.where(me < n - 1, drecv[step, 1, 0:3, :], F32(0))]
         for c in range(3):
             rows = [disp[c][h:h + 1, :] for h in range(8)] + [ghost[0][c:c + 1, :], ghost[1][c:c + 1, :]]
@@ -127,13 +148,11 @@
         for k in range(2):
             for c in range(3):
                 fsend[step, k, c:c + 1, :] = total[16 * c + 8 + k:16 * c + 9 + k, :]
-        for cp in force_copies(step):
-            cp.start()
+        start_both(force_copies(step)[::-1])
         return [total[16 * c:16 * c + 8, :] for c in range(3)]
 
     def advance(step, own, ext, disp, vel):
-        for cp in force_copies(step):
-            cp.wait()
+        wait_both(force_copies(step)[::-1])
         got = [jnp.where(me > 0, frecv[step, 0, 0:3, :], F32(0)), jnp.where(me < n - 1, frecv[step, 1, 0:3, :], F32(0))]
         parts = []
         for c in range(3):
@@ -165,15 +184,20 @@
     kcopy.wait()
     own = internal(0, disp)
 
-    def fwd_wait(i, _):
-        fwd(i).wait()
-        return 0
-    lax.fori_loop(1, n, fwd_wait, 0)
 
     sub128h = lax.broadcasted_iota(jnp.int32, (128, 128), 0).astype(jnp.int16)
 
-    def gather_load(t, acc):
-        base = pl.multiple_of(t * 8, 8)
+    tiles = n // 8
+    mine = me // 8
+
+    def gather_load(k, acc):
+        base = pl.multiple_of(lax.rem(mine + tiles - k, tiles) * 8, 8)
+        for s in range(8):
+            i = lax.rem(me + n - (base + s), n)
+
+            @pl.when(i != 0)
+            def _():
+                fwd(i).wait_recv()
         get = lambda r: recv[pl.ds(base, 8), r, :]
         loads = []
         for c in range(3):
@@ -194,7 +218,7 @@
                 v_x[:, at:at + 128] = jnp.concatenate(
                     [jnp.where(mask, jnp.broadcast_to(p[s:s + 1, :], (8, 128)), F32(0)) for p in highs + lows], axis=0).astype(BF16)
         return acc + lax.dot_general(v_x[...], oh_x[...], (((1,), (1,)), ((), ())), preferred_element_type=F32)
-    both = lax.fori_loop(0, n // 8, gather_load, jnp.zeros((48, 128), F32))
+    both = lax.fori_loop(0, tiles, gather_load, jnp.zeros((48, 128), F32))
     ext = [both[8 * c:8 * c + 8] + both[24 + 8 * c:32 + 8 * c] for c in range(3)]
 
     disp, vel = advance(0, own, ext, disp, vel)
@@ -207,42 +231,41 @@
             nd_ref[c:c + 1, 128 * h:128 * h + 128] = disp[c][h:h + 1, :]
             u_s[c, h:h + 1, 0:128] = disp[c][h:h + 1, :]
 
-    def back(t):
-        base = pl.multiple_of(t * 8, 8)
-        idx = [ids[j, pl.ds(base, 8), :] for j in range(4)]
-        for c in range(3):
-            p0 = p1 = q0 = q1 = jnp.zeros((8, 128), F32)
-            for j in range(4):
-                lo, hi = idx[j] & 127, idx[j] >> 7
-                acc = lane_take(jnp.broadcast_to(u_s[c, 0:1, 0:128], (8, 128)), lo)
-                for h in range(1, 8):
-                    acc = jnp.where(hi == h, lane_take(jnp.broadcast_to(u_s[c, h:h + 1, 0:128], (8, 128)), lo), acc)
-                p0 = p0 + weights[j][0] * acc
-                q0 = q0 + weights[j][1] * acc
-                p1 = p1 + weights[j][2] * acc
-                q1 = q1 + weights[j][3] * acc
-            outb[pl.ds(base, 8), 2 * c, :] = p0 + pltpu.roll(q0, 64, 1)
-            outb[pl.ds(base, 8), 2 * c + 1, :] = p1 + pltpu.roll(q1, 64, 1)
-
-    def back_loop(t, _):
-        back(t)
-        return 0
-    lax.fori_loop(0, n // 8, back_loop, 0)
-
     def ret(i):
         t = lax.rem(me + i, n)
         return near(outb.at[t], ret_ref.at[me], rs_sem.at[i], rr_sem.at[i], t)
 
-    def ret_start(i, _):
-        ret(i).start()
+    def back(k, _):
+        base = pl.multiple_of(lax.rem(mine + k, tiles) * 8, 8)
+        sums = [[jnp.zeros((8, 128), F32)] * 4 for c in range(3)]
+        for j in range(4):
+            idx = ids[j, pl.ds(base, 8), :]
+            lo, hi = idx & 127, idx >> 7
+            masks = [hi == h for h in range(1, 8)]
+            for c in range(3):
+                acc = lane_take(jnp.broadcast_to(u_s[c, 0:1, 0:128], (8, 128)), lo)
+                for h in range(1, 8):
+                    acc = jnp.where(masks[h - 1], lane_take(jnp.broadcast_to(u_s[c, h:h + 1, 0:128], (8, 128)), lo), acc)
+                sums[c] = [sums[c][m] + weights[j][m] * acc for m in range(4)]
+        for c in range(3):
+            p0, q0, p1, q1 = sums[c]
+            outb[pl.ds(base, 8), 2 * c, :] = p0 + pltpu.roll(q0, 64, 1)
+            outb[pl.ds(base, 8), 2 * c + 1, :] = p1 + pltpu.roll(q1, 64, 1)
+        for s in range(8):
+            i = lax.rem(base + s + n - me, n)
+
+            @pl.when(i != 0)
+            def _():
+                ret(i).start()
         return 0
-    lax.fori_loop(1, n, ret_start, 0)
+    lax.fori_loop(0, tiles, back, 0)
     ret_ref[me] = outb[me]
 
-    def ret_wait(i, _):
+    def drain(i, _):
+        fwd(i).wait_send()
         ret(i).wait()
         return 0
-    lax.fori_loop(1, n, ret_wait, 0)
+    lax.fori_loop(1, n, drain, 0)
 
 
 def solid(send, stiffness, connect, halo, mass, disp, vel, nx, ny, shapes):

time: 127 us -> 115 us (0.906)
  Pallas kernels: 103 us -> 91.2 us
    pallas_call x1, Pallas kernels: 86.5 us -> 74.5 us  [solid(): pl.pallas_call(functools.partial(solid_kernel, nx, ny, shapes), out_shape...]
where the time goes in v1:
time: 115 us
  Pallas kernels  91.2 us (79%)
  matrix products  10.7 us (9%)
  local copies, waits for them, and re-layouts  10.2 us (9%)
  other arithmetic  1.83 us (2%)
    pallas_call x1, Pallas kernels, solid(): pl.pallas_call(functools.partial(solid_kernel, nx, ny, shapes), out_shape...  74.5 us
    pallas_call x1, Pallas kernels, stencil(): pl.pallas_call(stencil_kernel, out_shape=jax.ShapeDtypeStruct((12, 4096),...  16.7 us
    dot_general x1, matrix products, spread_cols(): lax.dot_general(masked, upper_hot, (((1,), (1,)), ((), ())), precision=la...  5.72 us
    unnamed x31, local copies, waits for them, and re-layouts  4.36 us
    dot_general x1, matrix products, pick_cols(): lax.dot_general(grid, upper_hot, (((0,), (0,)), ((), ())), precision=lax....  4.07 us

profile of v1, /device:TPU:1, one launch (start us, length us, event | category | flops | bytes accessed | tf_op | source)
XLA Modules:
  0.0 114.9 jit_solution(13695740692475555907)
XLA Ops:
  0.6 0.5 broadcast.110
  1.1 1.4 %fusion.24 = (s32[4096]{0:T(1024)S(1)}, s32[4096,1]{0,1:T(1,128)S(1)}) fusion(s32[4096,1]{0,1:T(1,128)} %param.18, s32[]{:T(128)} %broadcast.110), kind=kLoop, calls=%fused_computation.33 | loop fusion | flops 4096 | bytes 49156 | tf_op args[5]
  2.6 0.3 convert_reduce_fusion
  2.9 0.0 copy-start.1
  2.9 0.0 copy-start.2
  2.9 0.0 copy-start.3
  2.9 0.0 copy-start.4
  2.9 0.0 copy-start.5
  2.9 1.0 fusion.7
  4.0 0.0 copy-start.12
  4.0 0.5 copy-done.1
  4.5 0.1 copy-done.2
  4.6 0.2 copy-done.3
  4.7 0.1 copy-done.4
  4.8 0.0 copy-done.5
  4.8 16.7 %stencil.1 = f32[12,4096]{1,0:T(8,128)S(1)} custom-call(s32[4096]{0:T(1024)S(1)} %copy-done.5, bf16[256,4096]{1,0:T(8,128)(2,1)S(1)} %copy-done.1, s32[32,4096]{1,0:T(8,128)S(1)} %copy-done.2, f32[32,4096]{1,0:T(8,128)S(1)} %copy-done.3, f32[12,4096]{1,0:T(8,128)S(1)} %copy-done.4), custom_call_target="tpu_custom_call" | custom-call | tf_op jit(solution)/shard_map/stencil/pallas_call | solution.py:359
  21.6 5.7 %fusion.12 = f32[20,256,32]{1,2,0:T(8,128)S(1)} fusion(s32[4096]{0:T(1024)S(1)} %get-tuple-element.7, f32[32,4096]{1,0:T(8,128)S(1)} %fusion.20, f32[20,4096]{1,0:T(8,128)S(1)} %pad_maximum_fusion), kind=kOutput, calls=%fused_computation.15 | convolution fusion | flops 8056733696 | bytes 1523712 | tf_op jit(solution)/shard_map/dot_general | solution.py:439
  27.3 0.9 copy.20
  28.2 1.5 %reshape_reshape.6 = f32[10,2,128,64]{3,2,1,0:T(8,128)} reshape(f32[20,256,32]{2,1,0:T(8,128)S(1)} %copy.20) | data formatting | bytes 1310720 | tf_op jit(solution)/shard_map/reshape;reshape | solution.py:499
  29.7 0.0 copy-start.9
  29.7 1.8 %copy.21 = f32[128,10,2,64]{0,3,2,1:T(8,128)S(1)} copy(f32[128,10,2,64]{3,0,2,1:T(8,128)} %bitcast.36) | data formatting | bytes 1310720 | tf_op jit(solution)/shard_map/transpose | solution.py:499
  31.5 0.5 copy.22.s_ref
  32.0 0.0 copy-start
  32.1 2.1 %copy-done = f32[60,60,256]{2,1,0:T(8,128)S(1)} copy-done((f32[60,60,256]{2,1,0:T(8,128)S(1)}, f32[60,60,256]{2,1,0:T(8,128)}, u32[]{:S(2)}) %copy-start) | copy-done | bytes 3686424
  34.2 74.5 %solid.1 = (f32[3,1024]{1,0:T(4,128)S(1)}, f32[128,6,128]{2,1,0:T(8,128)S(1)}) custom-call(f32[128,10,128]{2,1,0:T(8,128)S(1)} %copy.22.s_ref, f32[60,60,256]{2,1,0:T(8,128)S(1)} %copy-done, s32[24,256]{1,0:T(8,128)S(1)} %pad.4.con_ref, s32[2,128]{1,0:T(2,128)S(1)} %copy-done.9, f32[1,1024]{1,0:T(1,128)S(1)} %bitcast.34, f32[3,1024]{1,0:T(4,128)S(1)} %copy-done.6, ...), custom_call_target="tpu_custom_call" | custom-call | tf_op jit(solution)/shard_map/solid/pallas_call | solution.py:277
  108.7 0.2 copy.23
  108.9 0.3 copy.24
  109.1 0.3 reshape_reshape.7
  109.4 0.4 copy.25
  109.9 0.3 copy-done.11
  110.2 4.1 %multiply_reduce_fusion = f32[12,4096]{1,0:T(8,128)} fusion(f32[32,4096]{1,0:T(8,128)S(1)} %copy-done.11, s32[4096]{0:T(1024)S(1)} %get-tuple-element.7, f32[256,12,32]{0,2,1:T(8,128)S(1)} %copy.25), kind=kOutput, calls=%fused_computation.2 | convolution fusion | flops 4835983360 | bytes 1130496 | tf_op jit(solution)/shard_map/dot_general | solution.py:423
  114.3 0.6 copy.28
  (23 shorter events, 0.2 us)
Async XLA Ops:
  2.9 1.6 %copy-start.1 = (bf16[256,4096]{1,0:T(8,128)(2,1)S(1)}, bf16[256,4096]{1,0:T(8,128)(2,1)}, u32[]{:S(2)}) copy-start(bf16[256,4096]{1,0:T(8,128)(2,1)} %pr_ref.1) | copy-start | bytes 6291460
  2.9 1.7 %copy-start.2 = (s32[32,4096]{1,0:T(8,128)S(1)}, s32[32,4096]{1,0:T(8,128)}, u32[]{:S(2)}) copy-start(s32[32,4096]{1,0:T(8,128)} %loc_ref.1) | copy-start | bytes 1572868
  2.9 1.8 %copy-start.3 = (f32[32,4096]{1,0:T(8,128)S(1)}, f32[32,4096]{1,0:T(8,128)}, u32[]{:S(2)}) copy-start(f32[32,4096]{1,0:T(8,128)} %w_ref.1) | copy-start | bytes 1572868
  2.9 1.9 %copy-start.4 = (f32[12,4096]{1,0:T(8,128)S(1)}, f32[12,4096]{1,0:T(8,128)}, u32[]{:S(2)}) copy-start(f32[12,4096]{1,0:T(8,128)} %an_ref.1) | copy-start | bytes 589828
  2.9 1.9 %copy-start.5 = (s32[4096]{0:T(1024)S(1)}, s32[4096]{0:T(1024)}, u32[]{:S(2)}) copy-start(s32[4096]{0:T(1024)} %fb_ref.1) | copy-start | bytes 49156
  4.0 17.6 %copy-start.12 = (s32[8,4096]{1,0:T(8,128)S(1)}, s32[8,4096]{1,0:T(8,128)}, u32[]{:S(2)}) copy-start(s32[8,4096]{1,0:T(8,128)} %param.19) | copy-start | bytes 393220
  4.0 17.6 %copy-start.10 = (f32[32,4096]{1,0:T(8,128)}, f32[32,4096]{1,0:T(8,128)S(1)}, u32[]{:S(2)}) copy-start(f32[32,4096]{1,0:T(8,128)S(1)} %fusion.20) | copy-start | bytes 1572868
  29.7 2.3 %copy-start.13 = (s32[20,256]{1,0:T(8,128)S(1)}, s32[20,256]{1,0:T(8,128)}, u32[]{:S(2)}) copy-start(s32[20,256]{1,0:T(8,128)} %param.21) | copy-start | bytes 61444
  29.7 2.3 %copy-start.6 = (f32[3,1024]{1,0:T(4,128)S(1)}, f32[3,1024]{1,0:T(4,128)}, u32[]{:S(2)}) copy-start(f32[3,1024]{1,0:T(4,128)} %disp_ref.1) | copy-start | bytes 36868
  29.7 2.3 %copy-start.7 = (f32[3,1024]{1,0:T(4,128)S(1)}, f32[3,1024]{1,0:T(4,128)}, u32[]{:S(2)}) copy-start(f32[3,1024]{1,0:T(4,128)} %vel_ref.1) | copy-start | bytes 36868
  29.7 2.3 %copy-start.8 = (f32[1024]{0:T(1024)S(1)}, f32[1024]{0:T(1024)}, u32[]{:S(2)}) copy-start(f32[1024]{0:T(1024)} %param.23) | copy-start | bytes 12292
  29.7 2.3 %copy-start.9 = (s32[2,128]{1,0:T(2,128)S(1)}, s32[2,128]{1,0:T(2,128)}, u32[]{:S(2)}) copy-start(s32[2,128]{1,0:T(2,128)} %halo_ref.1) | copy-start | bytes 3076
  32.0 2.1 %copy-start = (f32[60,60,256]{2,1,0:T(8,128)S(1)}, f32[60,60,256]{2,1,0:T(8,128)}, u32[]{:S(2)}) copy-start(f32[60,60,256]{2,1,0:T(8,128)} %k_hbm.1) | copy-start | bytes 11059204
  109.1 1.0 copy-start.11

commit v2 on v1

--- a/solution.py
+++ b/solution.py
@@ -28,11 +28,139 @@
             half_lanes(pick(2, e), pick(3, o)), half_lanes(pick(3, e), pick(2, o))))
     return out
 
-def solid_kernel(nx, ny, shapes, s_ref, k_hbm, con_ref, halo_ref, mass_ref, disp_ref, vel_ref,
-                 nd_ref, ret_ref,
+STRIDE = 40
+UNR = 32
+TAKE = lax.GatherDimensionNumbers(
+    offset_dims=(), collapsed_slice_dims=(1,), start_index_map=(1,), operand_batching_dims=(0,), start_indices_batching_dims=(0,)
+)
+
+def lane_take(x, idx):
+    return lax.gather(x, idx[..., None], TAKE, slice_sizes=(1, 1), mode=lax.GatherScatterMode.PROMISE_IN_BOUNDS)
+
+def stencil_part(fb_ref, pr_ref, loc_ref, w_ref, an_ref, out_ref, tab32, tab, idxt, wt, res, arrive_lists, arrive_blocks):
+    arrive_lists()
+    for i in range(8):
+        idxt[128 * i:128 * i + 128, :] = jnp.concatenate(
+            [loc_ref[:, a * 1024 + 128 * i:a * 1024 + 128 * i + 128] for a in range(4)], axis=0).T
+        wt[128 * i:128 * i + 128, :] = jnp.concatenate(
+            [w_ref[:, a * 1024 + 128 * i:a * 1024 + 128 * i + 128] for a in range(4)], axis=0).T
+    arrive_blocks()
+
+    def relayout(b, _):
+        r0 = pl.multiple_of(b * 16, 16)
+        for t in range(32):
+            x = pr_ref[pl.ds(r0, 16), 128 * t:128 * t + 128].astype(jnp.float32)
+            tab32[pl.ds(t, 8, stride=STRIDE), :] = x[:8]
+            tab32[pl.ds(8 * STRIDE + t, 8, stride=STRIDE), :] = x[8:]
+        for n in range(16):
+            tab[r0 + n] = tab32[n * STRIDE:n * STRIDE + 32, :].astype(jnp.bfloat16)
+        return 0
+    lax.fori_loop(0, 16, relayout, 0)
+    lane = lax.broadcasted_iota(jnp.int32, (16, 128), 1)
+    sub = lax.broadcasted_iota(jnp.int32, (16, 128), 0).astype(jnp.int16)
+    grp = (lane // 32).astype(jnp.int16)
+    m_lo = grp < 2
+    m0 = grp == 0
+    m2 = grp == 2
+
+    def main(gg, _):
+        for uu in range(UNR // 8):
+            base = pl.multiple_of(gg * UNR + 8 * uu, 8)
+            rows = []
+            for u in range(8):
+                g = base + u
+                row = jnp.broadcast_to(idxt[pl.ds(g, 1), :], (16, 128))
+                lo = (row & 127).astype(jnp.int16)
+                hi = (row >> 7).astype(jnp.int16)
+                cl = hi < 16
+                mine = (hi & 15) == sub
+                xs = []
+                for a in range(4):
+                    block = tab[fb_ref[a * 1024 + g]]
+                    xs.append(jnp.where(cl, lane_take(block[:16], lo), lane_take(block[16:], lo)))
+                x = jnp.where(m_lo, jnp.where(m0, xs[0], xs[1]), jnp.where(m2, xs[2], xs[3]))
+                x = jnp.where(mine, x, jnp.bfloat16(0)).astype(jnp.float32)
+                rows.append(jnp.sum(x[:8] + x[8:], axis=0, keepdims=True))
+            res[pl.ds(base, 8), :] = jnp.concatenate(rows, axis=0) * wt[pl.ds(base, 8), :]
+        return 0
+    lax.fori_loop(0, 1024 // UNR, main, 0)
+    for i in range(8):
+        rt = res[128 * i:128 * i + 128, :].T
+        for a in range(4):
+            f0 = a * 1024 + 128 * i
+            fp = jnp.concatenate([jnp.sum(rt[a * 32 + 8 * q:a * 32 + 8 * q + 8], axis=0, keepdims=True) for q in range(4)], axis=0)
+            fp3 = jnp.concatenate([fp, fp, fp], axis=0)
+            out_ref[:, f0:f0 + 128] = -(an_ref[:, f0:f0 + 128] * fp3)
+
+
+def pack_part(tgt_ref, fn_ref, trac, slot_s, carry, acc, send_ref):
+    rows128 = lax.broadcasted_iota(jnp.int32, (128, 256), 0)
+    rows256 = lax.broadcasted_iota(jnp.int32, (256, 256), 0)
+    cols256 = lax.broadcasted_iota(jnp.int32, (256, 256), 1)
+    rows32 = lax.broadcasted_iota(jnp.int32, (32, 256), 0)
+    one_if = lambda m: jnp.where(m, F32(1), F32(0)).astype(BF16)
+    upper = one_if(rows256 < cols256)
+    ones = jnp.ones((256, 256), BF16)
+    carry[...] = jnp.zeros_like(carry)
+    acc[...] = jnp.zeros_like(acc)
+
+    def tile(kt, _):
+        at = pl.ds(pl.multiple_of(kt * 256, 256), 256)
+        target = tgt_ref[:, at]
+        hit = jnp.broadcast_to(target, (128, 256)) == rows128
+        hot = one_if(hit)
+        before = jnp.dot(hot, upper, preferred_element_type=F32) + carry[...]
+        carry[...] += jnp.dot(hot, ones, preferred_element_type=F32)
+        slot = jnp.sum(jnp.where(hit, before, F32(0)), axis=0, keepdims=True).astype(jnp.int32)
+        slot_s[:, at] = slot
+        place = jnp.broadcast_to(target + 128 * (slot >> 5), (256, 256))
+        weights = one_if(place == rows256)
+        mask = jnp.broadcast_to(slot & 31, (32, 256)) == rows32
+        values = [trac[:, at], fn_ref[:, at].astype(F32)]
+        total = None
+        highs = [v.astype(BF16).astype(F32) for v in values]
+        for part in (highs, [v - h for v, h in zip(values, highs)]):
+            x = [
+                jnp.where(mask, jnp.broadcast_to(p[r:r + 1, :], (32, 256)), F32(0)).astype(BF16)
+                for p in part
+                for r in range(p.shape[0])
+            ]
+            y = lax.dot_general(jnp.concatenate(x, axis=0), weights, (((1,), (1,)), ((), ())), preferred_element_type=F32)
+            total = y if total is None else total + y
+        acc[...] += total
+        return 0
+    lax.fori_loop(0, 16, tile, 0)
+    for r in range(10):
+        block = [acc[32 * v:32 * v + 32, 128 * h:128 * h + 128] for v in (2 * r, 2 * r + 1) for h in range(2)]
+        send_ref[:, r, :] = jnp.concatenate(block, axis=0).T
+
+
+def unpack_part(tgt_ref, slot_s, ret_ref, lhs, fd_ref):
+    rows128 = lax.broadcasted_iota(jnp.int32, (128, 256), 0)
+    rows64 = lax.broadcasted_iota(jnp.int32, (64, 256), 0)
+    for r in range(6):
+        x = ret_ref[:, r, :].T
+        xh = x.astype(BF16).astype(F32)
+        lhs[128 * r:128 * r + 128, :] = jnp.concatenate([xh, x - xh], axis=1).astype(BF16)
+
+    def tile(kt, _):
+        at = pl.ds(pl.multiple_of(kt * 256, 256), 256)
+        hot = jnp.where(jnp.broadcast_to(tgt_ref[:, at], (128, 256)) == rows128, F32(1), F32(0)).astype(BF16)
+        y = jnp.dot(lhs[...], jnp.concatenate([hot, hot], axis=0), preferred_element_type=F32)
+        mask = jnp.broadcast_to(slot_s[:, at], (64, 256)) == rows64
+        fd_ref[:, at] = jnp.concatenate(
+            [jnp.sum(jnp.where(mask, y[64 * v:64 * v + 64, :], F32(0)), axis=0, keepdims=True) for v in range(12)], axis=0
+        )
+        return 0
+    lax.fori_loop(0, 16, tile, 0)
+
+
+def solid_kernel(nx, ny, shapes, fb_ref, pr_hbm, loc_hbm, w_hbm, an_hbm, fn_hbm, tgt_ref, k_hbm, con_ref, halo_ref, mass_ref, disp_ref, vel_ref,
+                 nd_ref, fd_ref,
+                 pr_ref, loc_ref, w_ref, an_ref, fn_ref, trac, tab32, tab, idxt, wt, res, slot_s, carry, acc_s, s_ref, ret_ref, lhs,
                  recv, outb, kmat, ids, con_lo, con_hi, u_s, fh_s, fl_s, v_s, oh_e, oh_h, oh_x, v_x,
                  dsend, drecv, fsend, frecv,
-                 k_sem, fs_sem, fr_sem, rs_sem, rr_sem, ds_sem, dr_sem, gs_sem, gr_sem):
+                 in_sem, k_sem, fs_sem, fr_sem, rs_sem, rr_sem, ds_sem, dr_sem, gs_sem, gr_sem):
     n = nx * ny
     gx = lax.axis_index("gx")
     yz = lax.axis_index("yz")
@@ -40,6 +168,10 @@
     dev = lambda t: (t // ny, lax.rem(t, ny))
     nxt = lax.rem(me + 1, n)
     prv = lax.rem(me + n - 1, n)
+    ins = [pltpu.make_async_copy(src, dst, in_sem.at[k]) for k, (src, dst) in enumerate(
+        ((loc_hbm, loc_ref), (w_hbm, w_ref), (pr_hbm, pr_ref), (an_hbm, an_ref), (fn_hbm, fn_ref)))]
+    for cp in ins:
+        cp.start()
     kcopy = pltpu.make_async_copy(k_hbm, kmat, k_sem)
     kcopy.start()
     barrier = pltpu.get_barrier_semaphore()
@@ -53,22 +185,22 @@
     sub128 = lax.broadcasted_iota(jnp.int32, (128, 128), 0)
     weights = mix_weights(shapes)
 
-    con_lo[...] = con_ref[...] & 127
-    con_hi[...] = con_ref[...] >> 7
-    for a in range(20):
-        for e in range(2):
-            row = jnp.broadcast_to(con_lo[a:a + 1, 128 * e:128 * e + 128], (128, 128))
-            oh_e[a * 256 + 128 * e:a * 256 + 128 * e + 128, :] = jnp.where(row == sub128, F32(1), F32(0)).T.astype(BF16)
     halo_lo = [jnp.broadcast_to(halo_ref[r:r + 1, :] & 127, (8, 128)) for r in range(2)]
     halo_hi = [jnp.broadcast_to(halo_ref[r:r + 1, :] >> 7, (8, 128)) for r in range(2)]
-    for r in range(2):
-        row = jnp.broadcast_to(halo_ref[r:r + 1, :] & 127, (128, 128))
-        oh_h[128 * r:128 * r + 128, :] = jnp.where(row == sub128, F32(1), F32(0)).T.astype(BF16)
     stack = lambda ref, c: jnp.concatenate([ref[c:c + 1, 128 * h:128 * h + 128] for h in range(8)], axis=0)
     disp = [stack(disp_ref, c) for c in range(3)]
     vel = [stack(vel_ref, c) for c in range(3)]
     mass = stack(mass_ref, 0)
 
+    def arrive_lists():
+        ins[0].wait()
+        ins[1].wait()
+
+    def arrive_blocks():
+        for cp in ins[2:]:
+            cp.wait()
+    stencil_part(fb_ref, pr_ref, loc_ref, w_ref, an_ref, trac, tab32, tab, idxt, wt, res, arrive_lists, arrive_blocks)
+    pack_part(tgt_ref, fn_ref, trac, slot_s, carry, acc_s, s_ref)
     pl.semaphore_wait(barrier, n - 1)
 
     def near(src, dst, ss, rs, t):
@@ -181,6 +313,17 @@
         return 0
     lax.fori_loop(1, n, fwd_start, 0)
     recv[me] = s_ref[me]
+    for dst in (con_lo, con_hi):
+        dst[16:24, :] = jnp.zeros((8, 256), jnp.int32)
+    con_lo[0:20, :] = con_ref[...] & 127
+    con_hi[0:20, :] = con_ref[...] >> 7
+    for a in range(20):
+        for e in range(2):
+            row = jnp.broadcast_to(con_lo[a:a + 1, 128 * e:128 * e + 128], (128, 128))
+            oh_e[a * 256 + 128 * e:a * 256 + 128 * e + 128, :] = jnp.where(row == sub128, F32(1), F32(0)).T.astype(BF16)
+    for r in range(2):
+        row = jnp.broadcast_to(halo_ref[r:r + 1, :] & 127, (128, 128))
+        oh_h[128 * r:128 * r + 128, :] = jnp.where(row == sub128, F32(1), F32(0)).T.astype(BF16)
     kcopy.wait()
     own = internal(0, disp)
 
@@ -266,106 +409,37 @@
         ret(i).wait()
         return 0
     lax.fori_loop(1, n, drain, 0)
-
-
-def solid(send, stiffness, connect, halo, mass, disp, vel, nx, ny, shapes):
+    unpack_part(tgt_ref, slot_s, ret_ref, lhs, fd_ref)
+
+
+def solid(face_block, pressure, local, weight, area, nodes, target, stiffness, connect, halo, mass, disp, vel, nx, ny, shapes):
     n = nx * ny
     V = pl.BlockSpec(memory_space=pltpu.VMEM)
     A = pl.BlockSpec(memory_space=pl.ANY)
     D = pltpu.SemaphoreType.DMA
-    connect = jnp.pad(connect, ((0, 4), (0, 0)))
+    M = pltpu.VMEM
+    I32 = jnp.int32
     return pl.pallas_call(
         functools.partial(solid_kernel, nx, ny, shapes),
-        out_shape=(jax.ShapeDtypeStruct(disp.shape, F32), jax.ShapeDtypeStruct((n, 6, 128), F32)),
-        in_specs=[V, A, V, V, V, V, V],
+        out_shape=(jax.ShapeDtypeStruct(disp.shape, F32), jax.ShapeDtypeStruct((12, target.shape[1]), F32)),
+        in_specs=[pl.BlockSpec(memory_space=pltpu.SMEM), A, A, A, A, A, V, A, V, V, V, V, V],
         out_specs=(V, V),
         scratch_shapes=[
-            pltpu.VMEM((n, 10, 128), F32), pltpu.VMEM((n, 6, 128), F32), pltpu.VMEM((60, 60, 256), F32),
-            pltpu.VMEM((4, n, 128), jnp.int32), pltpu.VMEM((24, 256), jnp.int32), pltpu.VMEM((24, 256), jnp.int32),
-            pltpu.VMEM((3, 24, 256), F32), pltpu.VMEM((60, 256), F32), pltpu.VMEM((60, 256), F32),
-            pltpu.VMEM((96, 5120), BF16), pltpu.VMEM((5120, 128), BF16), pltpu.VMEM((256, 128), BF16),
-            pltpu.VMEM((128, 4096), BF16), pltpu.VMEM((48, 4096), BF16),
-            pltpu.VMEM((SUBSTEPS, 2, 8, 128), F32), pltpu.VMEM((SUBSTEPS, 2, 8, 128), F32),
-            pltpu.VMEM((SUBSTEPS, 2, 8, 128), F32), pltpu.VMEM((SUBSTEPS, 2, 8, 128), F32),
-            D, D((n,)), D((n,)), D((n,)), D((n,)), D((SUBSTEPS, 2)), D((SUBSTEPS, 2)), D((SUBSTEPS, 2)), D((SUBSTEPS, 2))],
-        compiler_params=pltpu.CompilerParams(collective_id=0, has_side_effects=True, vmem_limit_bytes=48 * 2**20),
+            M(pressure.shape, BF16), M(local.shape, I32), M(weight.shape, F32), M(area.shape, F32), M(nodes.shape, I32),
+            M(area.shape, F32), M((16 * STRIDE, 128), F32), M((256, 32, 128), BF16), M((1024, 128), I32), M((1024, 128), F32),
+            M((1024, 128), F32), M(target.shape, I32), M((128, 256), F32), M((640, 256), F32),
+            M((n, 10, 128), F32), M((n, 6, 128), F32), M((768, 256), BF16),
+            M((n, 10, 128), F32), M((n, 6, 128), F32), M((60, 60, 256), F32),
+            M((4, n, 128), I32), M((24, 256), I32), M((24, 256), I32),
+            M((3, 24, 256), F32), M((60, 256), F32), M((60, 256), F32),
+            M((96, 5120), BF16), M((5120, 128), BF16), M((256, 128), BF16),
+            M((128, 4096), BF16), M((48, 4096), BF16),
+            M((SUBSTEPS, 2, 8, 128), F32), M((SUBSTEPS, 2, 8, 128), F32),
+            M((SUBSTEPS, 2, 8, 128), F32), M((SUBSTEPS, 2, 8, 128), F32),
+            D((5,)), D, D((n,)), D((n,)), D((n,)), D((n,)), D((SUBSTEPS, 2)), D((SUBSTEPS, 2)), D((SUBSTEPS, 2)), D((SUBSTEPS, 2))],
+        compiler_params=pltpu.CompilerParams(collective_id=0, has_side_effects=True, vmem_limit_bytes=56 * 2**20),
         name="solid",
-    )(send, stiffness, connect, halo, mass.reshape(1, -1), disp, vel)
-
-
-STRIDE = 40
-UNR = 32
-TAKE = lax.GatherDimensionNumbers(
-    offset_dims=(), collapsed_slice_dims=(1,), start_index_map=(1,), operand_batching_dims=(0,), start_indices_batching_dims=(0,)
-)
-
-def lane_take(x, idx):
-    return lax.gather(x, idx[..., None], TAKE, slice_sizes=(1, 1), mode=lax.GatherScatterMode.PROMISE_IN_BOUNDS)
-
-def stencil_kernel(fb_ref, pr_ref, loc_ref, w_ref, an_ref, out_ref, tab32, tab, idxt, wt, res):
-    def relayout(b, _):
-        r0 = pl.multiple_of(b * 16, 16)
-        for t in range(32):
-            x = pr_ref[pl.ds(r0, 16), 128 * t:128 * t + 128].astype(jnp.float32)
-            tab32[pl.ds(t, 8, stride=STRIDE), :] = x[:8]
-            tab32[pl.ds(8 * STRIDE + t, 8, stride=STRIDE), :] = x[8:]
-        for n in range(16):
-            tab[pl.ds(pl.multiple_of((r0 + n) * 32, 32), 32), :] = tab32[n * STRIDE:n * STRIDE + 32, :].astype(jnp.bfloat16)
-        return 0
-    lax.fori_loop(0, 16, relayout, 0)
-    for i in range(8):
-        idxt[128 * i:128 * i + 128, :] = jnp.concatenate(
-            [loc_ref[:, a * 1024 + 128 * i:a * 1024 + 128 * i + 128] for a in range(4)], axis=0).T
-        wt[128 * i:128 * i + 128, :] = jnp.concatenate(
-            [w_ref[:, a * 1024 + 128 * i:a * 1024 + 128 * i + 128] for a in range(4)], axis=0).T
-    lane = lax.broadcasted_iota(jnp.int32, (16, 128), 1)
-    sub = lax.broadcasted_iota(jnp.int32, (16, 128), 0).astype(jnp.int16)
-    grp = (lane // 32).astype(jnp.int16)
-    m_lo = grp < 2
-    m0 = grp == 0
-    m2 = grp == 2
-
-    def main(gg, _):
-        for uu in range(UNR // 8):
-            base = pl.multiple_of(gg * UNR + 8 * uu, 8)
-            rows = []
-            for u in range(8):
-                g = base + u
-                row = jnp.broadcast_to(idxt[pl.ds(g, 1), :], (16, 128))
-                lo = (row & 127).astype(jnp.int16)
-                hi = (row >> 7).astype(jnp.int16)
-                cl = hi < 16
-                mine = (hi & 15) == sub
-                xs = []
-                for a in range(4):
-                    off = pl.multiple_of(fb_ref[a * 1024 + g] * 32, 32)
-                    xs.append(jnp.where(cl, lane_take(tab[pl.ds(off, 16), :], lo), lane_take(tab[pl.ds(off + 16, 16), :], lo)))
-                x = jnp.where(m_lo, jnp.where(m0, xs[0], xs[1]), jnp.where(m2, xs[2], xs[3]))
-                x = jnp.where(mine, x, jnp.bfloat16(0)).astype(jnp.float32)
-                rows.append(jnp.sum(x[:8] + x[8:], axis=0, keepdims=True))
-            res[pl.ds(base, 8), :] = jnp.concatenate(rows, axis=0) * wt[pl.ds(base, 8), :]
-        return 0
-    lax.fori_loop(0, 1024 // UNR, main, 0)
-    for i in range(8):
-        rt = res[128 * i:128 * i + 128, :].T
-        for a in range(4):
-            f0 = a * 1024 + 128 * i
-            fp = jnp.concatenate([jnp.sum(rt[a * 32 + 8 * q:a * 32 + 8 * q + 8], axis=0, keepdims=True) for q in range(4)], axis=0)
-            fp3 = jnp.concatenate([fp, fp, fp], axis=0)
-            out_ref[:, f0:f0 + 128] = -(an_ref[:, f0:f0 + 128] * fp3)
-
-def stencil(face_block, pressure, local, weight, area):
-    V = pl.BlockSpec(memory_space=pltpu.VMEM)
-    return pl.pallas_call(
-        stencil_kernel,
-        out_shape=jax.ShapeDtypeStruct((12, 4096), jnp.float32),
-        in_specs=[pl.BlockSpec(memory_space=pltpu.SMEM), V, V, V, V],
-        out_specs=V,
-        scratch_shapes=[pltpu.VMEM((16 * STRIDE, 128), jnp.float32), pltpu.VMEM((8192, 128), jnp.bfloat16), pltpu.VMEM((1024, 128), jnp.int32),
-                        pltpu.VMEM((1024, 128), jnp.float32), pltpu.VMEM((1024, 128), jnp.float32)],
-        compiler_params=pltpu.CompilerParams(vmem_limit_bytes=40 * 2**20),
-        name="stencil",
-    )(face_block, pressure, local, weight, area)
+    )(face_block, pressure, local, weight, area, nodes, target, stiffness, connect, halo, mass.reshape(1, -1), disp, vel)
 
 
 def shape_table():
@@ -398,76 +472,6 @@
     return shape_values
 
 
-def hot_pair(indices, extent):
-    lanes_width = 32
-    upper_count = -(-extent // lanes_width)
-    upper_hot = (
-        indices[None, :] // lanes_width == lax.broadcasted_iota(jnp.int32, (upper_count, 1), 0)
-    ).astype(jnp.float32)
-    lower_hot = (
-        indices[None, :] % lanes_width == lax.broadcasted_iota(jnp.int32, (lanes_width, 1), 0)
-    ).astype(jnp.float32)
-    return (upper_hot, lower_hot)
-
-
-def pick_cols(table, hots):
-    upper_hot, lower_hot = hots
-    lanes_width = lower_hot.shape[0]
-    upper_count = upper_hot.shape[0]
-    comps, extent = table.shape
-    grid = (
-        table.reshape(comps, upper_count, lanes_width)
-        .transpose(1, 0, 2)
-        .reshape(upper_count, comps * lanes_width)
-    )
-    rows_out = lax.dot_general(
-        grid,
-        upper_hot,
-        (((0,), (0,)), ((), ())),
-        precision=lax.Precision.HIGHEST,
-        preferred_element_type=jnp.float32,
-    )
-    return jnp.sum(rows_out.reshape(comps, lanes_width, -1) * lower_hot[None], axis=1)
-
-
-def spread_cols(values, hots):
-    upper_hot, lower_hot = hots
-    lanes_width = lower_hot.shape[0]
-    upper_count = upper_hot.shape[0]
-    comps = values.shape[0]
-    masked = (values[:, None, :] * lower_hot[None]).reshape(comps * lanes_width, -1)
-    summed = lax.dot_general(
-        masked,
-        upper_hot,
-        (((1,), (1,)), ((), ())),
-        precision=lax.Precision.HIGHEST,
-        preferred_element_type=jnp.float32,
-    )
-    return (
-        summed.reshape(comps, lanes_width, upper_count)
-        .transpose(0, 2, 1)
-        .reshape(comps, upper_count * lanes_width)
-    )
-
-
-def arrival_order(target, devices):
-    row_count = target.shape[0]
-    group_rows = min(512, row_count)
-    groups = row_count // group_rows
-    onehot = (target[:, None] == jnp.arange(devices, dtype=jnp.int32)[None, :]).astype(jnp.bfloat16)
-    onehot = onehot.reshape(groups, group_rows, devices)
-    lower_ones = (
-        lax.broadcasted_iota(jnp.int32, (group_rows, group_rows), 0)
-        > lax.broadcasted_iota(jnp.int32, (group_rows, group_rows), 1)
-    ).astype(jnp.bfloat16)
-    before = jnp.einsum("ij,gjd->gid", lower_ones, onehot, preferred_element_type=jnp.float32)
-    onehot_float = onehot.astype(jnp.float32)
-    totals = jnp.sum(onehot_float, axis=1)
-    offsets = jnp.cumsum(totals, axis=0) - totals
-    placed = jnp.sum((before + offsets[:, None, :]) * onehot_float, axis=2)
-    return placed.reshape(row_count).astype(jnp.int32)
-
-
 def shards(
     pressure,
     face_block,
@@ -485,24 +489,10 @@
 ):
     gx_size = lax.axis_size("gx")
     yz_size = lax.axis_size("yz")
-    devices = gx_size * yz_size
-    face_count = face_block.shape[0]
-    capacity = 2 * face_count // devices
-    slot_total = devices * capacity
-    traction = stencil(face_block, pressure, stencil_local, stencil_weight, area_normal)
-    target = face_part[:, 0]
-    slots = target * capacity + arrival_order(target, devices)
-    slot_hots = hot_pair(slots, slot_total)
-    packed = spread_cols(
-        jnp.concatenate([traction, face_nodes.astype(jnp.float32)], axis=0), slot_hots
+    return solid(
+        face_block, pressure, stencil_local, stencil_weight, area_normal, face_nodes, face_part.reshape(1, -1),
+        stiffness, connect, halo_nodes, node_mass, displacement, velocity, gx_size, yz_size, shape_table()
     )
-    send = packed.reshape(10, 2, devices, capacity).transpose(2, 0, 1, 3).reshape(devices, 10, 2 * capacity)
-    node_disp, returned = solid(
-        send, stiffness, connect, halo_nodes, node_mass, displacement, velocity, gx_size, yz_size, shape_table()
-    )
-    returned = returned.reshape(devices, 6, 2, capacity).transpose(1, 2, 0, 3).reshape(12, slot_total)
-    face_disp = pick_cols(returned, slot_hots)
-    return (node_disp, face_disp)
 
 
 def solution(mesh):

time: 115 us -> 107 us (0.930)
  Pallas kernels: 91.2 us -> 103 us
  matrix products: 10.7 us -> 0 us
  local copies, waits for them, and re-layouts: 10.2 us -> 3 us
  other arithmetic: 1.83 us -> 0 us
    pallas_call x1, Pallas kernels: 74.5 us -> 103 us  [solid(): pl.pallas_call(functools.partial(solid_kernel, nx, ny, shapes), out_shape...]
    pallas_call x1 -> x0, Pallas kernels: 16.7 us -> none  [stencil(): pl.pallas_call(stencil_kernel, out_shape=jax.ShapeDtypeStruct((12, 4096),...]
    dot_general x3 -> x0, matrix products: 10.7 us -> none  [the longest x1 5.72 us: spread_cols(): lax.dot_general(masked, upper_hot, (((1,), (1,)), ((), ())), precision=la...]
    transpose x4 -> x0, local copies, waits for them, and re-layouts: 3.36 us -> none  [the longest x1 1.75 us: shards(): packed.reshape(10, 2, devices, capacity).transpose(2, 0, 1, 3)]
    another operation x2 -> x0, local copies, waits for them, and re-layouts: 1.75 us -> none  [the longest x1 1.48 us: shards(): packed.reshape(10, 2, devices, capacity).transpose(2, 0, 1, 3)]
    unnamed x2 -> x0, other arithmetic: 1.41 us -> none
    unnamed x31 -> x2, local copies, waits for them, and re-layouts: 4.36 us -> 3 us
where the time goes in v2:
time: 107 us
  Pallas kernels  103 us (96%)
  local copies, waits for them, and re-layouts  3 us (3%)
    pallas_call x1, Pallas kernels, solid(): pl.pallas_call(functools.partial(solid_kernel, nx, ny, shapes), out_shape...  103 us
    unnamed x2, local copies, waits for them, and re-layouts  3 us

profile of v2, /device:TPU:1, one launch (start us, length us, event | category | flops | bytes accessed | tf_op | source)
XLA Modules:
  0.0 106.6 jit_solution(638785966226968864)
XLA Ops:
  0.6 103.0 %solid.1 = (f32[3,1024]{1,0:T(4,128)}, f32[12,4096]{1,0:T(8,128)}) custom-call(s32[4096]{0:T(1024)} %fb_ref.1, bf16[256,4096]{1,0:T(8,128)(2,1)} %pr_hbm.1, s32[32,4096]{1,0:T(8,128)} %loc_hbm.1, f32[32,4096]{1,0:T(8,128)} %w_hbm.1, f32[12,4096]{1,0:T(8,128)} %an_hbm.1, s32[8,4096]{1,0:T(8,128)} %fn_hbm.1, s32[1,4096]{1,0:T(1,128)} %bitcast.2, ...), custom_call_target="tpu_custom_call" | custom-call | tf_op jit(solution)/shard_map/solid/pallas_call | solution.py:422
  103.6 1.3 %copy.17 = f32[3,1024]{1,0:T(4,128)} copy(f32[3,1024]{1,0:T(4,128)} %get-tuple-element.4) | data formatting | bytes 24576
  104.9 1.7 %copy.18 = f32[12,4096]{1,0:T(8,128)} copy(f32[12,4096]{1,0:T(8,128)} %get-tuple-element.5) | data formatting | bytes 393216

commit v3 on v2

--- a/solution.py
+++ b/solution.py
@@ -94,34 +94,43 @@
 
 
 def pack_part(tgt_ref, fn_ref, trac, slot_s, carry, acc, send_ref):
+    wide = 1024
     rows128 = lax.broadcasted_iota(jnp.int32, (128, 256), 0)
     rows256 = lax.broadcasted_iota(jnp.int32, (256, 256), 0)
     cols256 = lax.broadcasted_iota(jnp.int32, (256, 256), 1)
-    rows32 = lax.broadcasted_iota(jnp.int32, (32, 256), 0)
+    rows256w = lax.broadcasted_iota(jnp.int32, (256, wide), 0)
+    rows32 = lax.broadcasted_iota(jnp.int32, (32, wide), 0)
     one_if = lambda m: jnp.where(m, F32(1), F32(0)).astype(BF16)
     upper = one_if(rows256 < cols256)
     ones = jnp.ones((256, 256), BF16)
     carry[...] = jnp.zeros_like(carry)
     acc[...] = jnp.zeros_like(acc)
 
+    def rank(kt, _):
+        before = carry[...]
+        for m in range(4):
+            at = pl.ds(pl.multiple_of(kt * wide + 256 * m, 256), 256)
+            hit = jnp.broadcast_to(tgt_ref[:, at], (128, 256)) == rows128
+            hot = one_if(hit)
+            within = jnp.dot(hot, upper, preferred_element_type=F32) + before
+            slot_s[:, at] = jnp.sum(jnp.where(hit, within, F32(0)), axis=0, keepdims=True).astype(jnp.int32)
+            before = before + jnp.dot(hot, ones, preferred_element_type=F32)
+        carry[...] = before
+        return 0
+    lax.fori_loop(0, 4, rank, 0)
+
     def tile(kt, _):
-        at = pl.ds(pl.multiple_of(kt * 256, 256), 256)
-        target = tgt_ref[:, at]
-        hit = jnp.broadcast_to(target, (128, 256)) == rows128
-        hot = one_if(hit)
-        before = jnp.dot(hot, upper, preferred_element_type=F32) + carry[...]
-        carry[...] += jnp.dot(hot, ones, preferred_element_type=F32)
-        slot = jnp.sum(jnp.where(hit, before, F32(0)), axis=0, keepdims=True).astype(jnp.int32)
-        slot_s[:, at] = slot
-        place = jnp.broadcast_to(target + 128 * (slot >> 5), (256, 256))
-        weights = one_if(place == rows256)
-        mask = jnp.broadcast_to(slot & 31, (32, 256)) == rows32
+        at = pl.ds(pl.multiple_of(kt * wide, wide), wide)
+        slot = slot_s[:, at]
+        place = jnp.broadcast_to(tgt_ref[:, at] + 128 * (slot >> 5), (256, wide))
+        weights = one_if(place == rows256w)
+        mask = jnp.broadcast_to(slot & 31, (32, wide)) == rows32
         values = [trac[:, at], fn_ref[:, at].astype(F32)]
         total = None
         highs = [v.astype(BF16).astype(F32) for v in values]
         for part in (highs, [v - h for v, h in zip(values, highs)]):
             x = [
-                jnp.where(mask, jnp.broadcast_to(p[r:r + 1, :], (32, 256)), F32(0)).astype(BF16)
+                jnp.where(mask, jnp.broadcast_to(p[r:r + 1, :], (32, wide)), F32(0)).astype(BF16)
                 for p in part
                 for r in range(p.shape[0])
             ]
@@ -129,36 +138,37 @@
             total = y if total is None else total + y
         acc[...] += total
         return 0
-    lax.fori_loop(0, 16, tile, 0)
+    lax.fori_loop(0, 4, tile, 0)
     for r in range(10):
         block = [acc[32 * v:32 * v + 32, 128 * h:128 * h + 128] for v in (2 * r, 2 * r + 1) for h in range(2)]
         send_ref[:, r, :] = jnp.concatenate(block, axis=0).T
 
 
 def unpack_part(tgt_ref, slot_s, ret_ref, lhs, fd_ref):
-    rows128 = lax.broadcasted_iota(jnp.int32, (128, 256), 0)
-    rows64 = lax.broadcasted_iota(jnp.int32, (64, 256), 0)
+    wide = 512
+    rows128 = lax.broadcasted_iota(jnp.int32, (128, wide), 0)
+    rows64 = lax.broadcasted_iota(jnp.int32, (64, wide), 0)
     for r in range(6):
         x = ret_ref[:, r, :].T
         xh = x.astype(BF16).astype(F32)
         lhs[128 * r:128 * r + 128, :] = jnp.concatenate([xh, x - xh], axis=1).astype(BF16)
 
     def tile(kt, _):
-        at = pl.ds(pl.multiple_of(kt * 256, 256), 256)
-        hot = jnp.where(jnp.broadcast_to(tgt_ref[:, at], (128, 256)) == rows128, F32(1), F32(0)).astype(BF16)
+        at = pl.ds(pl.multiple_of(kt * wide, wide), wide)
+        hot = jnp.where(jnp.broadcast_to(tgt_ref[:, at], (128, wide)) == rows128, F32(1), F32(0)).astype(BF16)
         y = jnp.dot(lhs[...], jnp.concatenate([hot, hot], axis=0), preferred_element_type=F32)
-        mask = jnp.broadcast_to(slot_s[:, at], (64, 256)) == rows64
+        mask = jnp.broadcast_to(slot_s[:, at], (64, wide)) == rows64
         fd_ref[:, at] = jnp.concatenate(
             [jnp.sum(jnp.where(mask, y[64 * v:64 * v + 64, :], F32(0)), axis=0, keepdims=True) for v in range(12)], axis=0
         )
         return 0
-    lax.fori_loop(0, 16, tile, 0)
+    lax.fori_loop(0, 8, tile, 0)
 
 
 def solid_kernel(nx, ny, shapes, fb_ref, pr_hbm, loc_hbm, w_hbm, an_hbm, fn_hbm, tgt_ref, k_hbm, con_ref, halo_ref, mass_ref, disp_ref, vel_ref,
                  nd_ref, fd_ref,
                  pr_ref, loc_ref, w_ref, an_ref, fn_ref, trac, tab32, tab, idxt, wt, res, slot_s, carry, acc_s, s_ref, ret_ref, lhs,
-                 recv, outb, kmat, ids, con_lo, con_hi, u_s, fh_s, fl_s, v_s, oh_e, oh_h, oh_x, v_x,
+                 recv, outb, kmat, ids, con_lo, con_hi, u_s, fh_s, fl_s, v_s, oh_e, oh_h,
                  dsend, drecv, fsend, frecv,
                  in_sem, k_sem, fs_sem, fr_sem, rs_sem, rr_sem, ds_sem, dr_sem, gs_sem, gr_sem):
     n = nx * ny
@@ -176,10 +186,16 @@
     kcopy.start()
     barrier = pltpu.get_barrier_semaphore()
 
-    def greet(i, _):
-        pl.semaphore_signal(barrier, inc=1, device_id=dev(lax.rem(me + i, n)), device_id_type=MESH)
-        return 0
-    lax.fori_loop(1, n, greet, 0)
+    gx_at = [lax.rem(gx + a, nx) for a in range(nx)]
+
+    def greet(b, _):
+        y = lax.rem(yz + b, ny)
+        for a in range(nx):
+            pl.semaphore_signal(barrier, inc=1, device_id=(gx_at[a], y), device_id_type=MESH)
+        return 0
+    lax.fori_loop(1, ny, greet, 0)
+    for a in range(1, nx):
+        pl.semaphore_signal(barrier, inc=1, device_id=(gx_at[a], yz), device_id_type=MESH)
 
     sub8 = lax.broadcasted_iota(jnp.int32, (8, 128), 0)
     sub128 = lax.broadcasted_iota(jnp.int32, (128, 128), 0)
@@ -304,14 +320,19 @@
 
     send_disp(0, disp)
 
-    def fwd(i):
-        t = lax.rem(me + i, n)
-        return near(s_ref.at[t], recv.at[me], fs_sem.at[i], fr_sem.at[i], t)
-
-    def fwd_start(i, _):
-        fwd(i).start()
-        return 0
-    lax.fori_loop(1, n, fwd_start, 0)
+    def fwd(a, b, g, y):
+        return pltpu.make_async_remote_copy(
+            src_ref=s_ref.at[g * ny + y], dst_ref=recv.at[me], send_sem=fs_sem.at[a * ny + b], recv_sem=fr_sem.at[a * ny + b],
+            device_id=(g, y), device_id_type=MESH)
+
+    def fwd_start(b, _):
+        y = lax.rem(yz + b, ny)
+        for a in range(nx):
+            fwd(a, b, gx_at[a], y).start()
+        return 0
+    lax.fori_loop(1, ny, fwd_start, 0)
+    for a in range(1, nx):
+        fwd(a, 0, gx_at[a], yz).start()
     recv[me] = s_ref[me]
     for dst in (con_lo, con_hi):
         dst[16:24, :] = jnp.zeros((8, 256), jnp.int32)
@@ -335,32 +356,37 @@
 
     def gather_load(k, acc):
         base = pl.multiple_of(lax.rem(mine + tiles - k, tiles) * 8, 8)
+        a = lax.rem(gx + nx - base // ny, nx)
         for s in range(8):
-            i = lax.rem(me + n - (base + s), n)
-
-            @pl.when(i != 0)
+            b = lax.rem(yz + ny - lax.rem(base, ny) - s, ny)
+
+            @pl.when(base + s != me)
             def _():
-                fwd(i).wait_recv()
+                fwd(a, b, gx, yz).wait_recv()
         get = lambda r: recv[pl.ds(base, 8), r, :]
         loads = []
         for c in range(3):
             t0, t1 = get(2 * c), get(2 * c + 1)
             r0, r1 = pltpu.roll(t0, 64, 1), pltpu.roll(t1, 64, 1)
             loads.append([weights[j][0] * t0 + weights[j][1] * r0 + weights[j][2] * t1 + weights[j][3] * r1 for j in range(4)])
+        total = jnp.zeros((48, 128), F32)
         for j in range(4):
             idx = get(6 + j).astype(jnp.int32)
             ids[j, pl.ds(base, 8), :] = idx
             lo, hi = idx & 127, idx >> 7
             highs = [loads[c][j].astype(BF16).astype(F32) for c in range(3)]
             lows = [loads[c][j] - highs[c] for c in range(3)]
-            for s in range(8):
-                at = (j * 8 + s) * 128
-                row = jnp.broadcast_to(lo[s:s + 1, :], (128, 128)).astype(jnp.int16)
-                oh_x[:, at:at + 128] = jnp.where(row == sub128h, BF16(1), BF16(0))
-                mask = jnp.broadcast_to(hi[s:s + 1, :], (8, 128)) == sub8
-                v_x[:, at:at + 128] = jnp.concatenate(
-                    [jnp.where(mask, jnp.broadcast_to(p[s:s + 1, :], (8, 128)), F32(0)) for p in highs + lows], axis=0).astype(BF16)
-        return acc + lax.dot_general(v_x[...], oh_x[...], (((1,), (1,)), ((), ())), preferred_element_type=F32)
+            for s in range(0, 8, 2):
+                hots, vals = [], []
+                for k in (s, s + 1):
+                    row = jnp.broadcast_to(lo[k:k + 1, :], (128, 128)).astype(jnp.int16)
+                    hots.append(jnp.where(row == sub128h, BF16(1), BF16(0)))
+                    mask = jnp.broadcast_to(hi[k:k + 1, :], (8, 128)) == sub8
+                    vals.append(jnp.concatenate(
+                        [jnp.where(mask, jnp.broadcast_to(p[k:k + 1, :], (8, 128)), F32(0)) for p in highs + lows], axis=0).astype(BF16))
+                total = total + lax.dot_general(
+                    jnp.concatenate(vals, axis=1), jnp.concatenate(hots, axis=1), (((1,), (1,)), ((), ())), preferred_element_type=F32)
+        return acc + total
     both = lax.fori_loop(0, tiles, gather_load, jnp.zeros((48, 128), F32))
     ext = [both[8 * c:8 * c + 8] + both[24 + 8 * c:32 + 8 * c] for c in range(3)]
 
@@ -405,7 +431,7 @@
     ret_ref[me] = outb[me]
 
     def drain(i, _):
-        fwd(i).wait_send()
+        fwd(i // ny, lax.rem(i, ny), gx, yz).wait_send()
         ret(i).wait()
         return 0
     lax.fori_loop(1, n, drain, 0)
@@ -433,7 +459,6 @@
             M((4, n, 128), I32), M((24, 256), I32), M((24, 256), I32),
             M((3, 24, 256), F32), M((60, 256), F32), M((60, 256), F32),
             M((96, 5120), BF16), M((5120, 128), BF16), M((256, 128), BF16),
-            M((128, 4096), BF16), M((48, 4096), BF16),
             M((SUBSTEPS, 2, 8, 128), F32), M((SUBSTEPS, 2, 8, 128), F32),
             M((SUBSTEPS, 2, 8, 128), F32), M((SUBSTEPS, 2, 8, 128), F32),
             D((5,)), D, D((n,)), D((n,)), D((n,)), D((n,)), D((SUBSTEPS, 2)), D((SUBSTEPS, 2)), D((SUBSTEPS, 2)), D((SUBSTEPS, 2))],

time: 107 us -> 100 us (0.935)
  Pallas kernels: 103 us -> 96.4 us
    pallas_call x1, Pallas kernels: 103 us -> 96.4 us  [solid(): pl.pallas_call(functools.partial(solid_kernel, nx, ny, shapes), out_shape...]
where the time goes in v3:
time: 100 us
  Pallas kernels  96.4 us (96%)
  local copies, waits for them, and re-layouts  3 us (3%)
    pallas_call x1, Pallas kernels, solid(): pl.pallas_call(functools.partial(solid_kernel, nx, ny, shapes), out_shape...  96.4 us
    unnamed x2, local copies, waits for them, and re-layouts  3 us

profile of v3, /device:TPU:1, one launch (start us, length us, event | category | flops | bytes accessed | tf_op | source)
XLA Modules:
  0.0 100.0 jit_solution(2258357788630829491)
XLA Ops:
  0.6 96.4 %solid.1 = (f32[3,1024]{1,0:T(4,128)}, f32[12,4096]{1,0:T(8,128)}) custom-call(s32[4096]{0:T(1024)} %fb_ref.1, bf16[256,4096]{1,0:T(8,128)(2,1)} %pr_hbm.1, s32[32,4096]{1,0:T(8,128)} %loc_hbm.1, f32[32,4096]{1,0:T(8,128)} %w_hbm.1, f32[12,4096]{1,0:T(8,128)} %an_hbm.1, s32[8,4096]{1,0:T(8,128)} %fn_hbm.1, s32[1,4096]{1,0:T(1,128)} %bitcast.2, ...), custom_call_target="tpu_custom_call" | custom-call | tf_op jit(solution)/shard_map/solid/pallas_call | solution.py:448
  97.0 1.3 %copy.17 = f32[3,1024]{1,0:T(4,128)} copy(f32[3,1024]{1,0:T(4,128)} %get-tuple-element.4) | data formatting | bytes 24576
  98.4 1.7 %copy.18 = f32[12,4096]{1,0:T(8,128)} copy(f32[12,4096]{1,0:T(8,128)} %get-tuple-element.5) | data formatting | bytes 393216

commit v4 on v3

--- a/solution.py
+++ b/solution.py
@@ -144,7 +144,8 @@
         send_ref[:, r, :] = jnp.concatenate(block, axis=0).T
 
 
-def unpack_part(tgt_ref, slot_s, ret_ref, lhs, fd_ref):
+def unpack_kernel(tgt_ref, slot_s, ret_ref, nd_in, nd_ref, fd_ref, lhs):
+    nd_ref[...] = nd_in[...]
     wide = 512
     rows128 = lax.broadcasted_iota(jnp.int32, (128, wide), 0)
     rows64 = lax.broadcasted_iota(jnp.int32, (64, wide), 0)
@@ -166,8 +167,8 @@
 
 
 def solid_kernel(nx, ny, shapes, fb_ref, pr_hbm, loc_hbm, w_hbm, an_hbm, fn_hbm, tgt_ref, k_hbm, con_ref, halo_ref, mass_ref, disp_ref, vel_ref,
-                 nd_ref, fd_ref,
-                 pr_ref, loc_ref, w_ref, an_ref, fn_ref, trac, tab32, tab, idxt, wt, res, slot_s, carry, acc_s, s_ref, ret_ref, lhs,
+                 nd_ref, ret_ref, slot_s,
+                 pr_ref, loc_ref, w_ref, an_ref, fn_ref, trac, tab32, tab, idxt, wt, res, carry, acc_s, s_ref,
                  recv, outb, kmat, ids, con_lo, con_hi, u_s, fh_s, fl_s, v_s, oh_e, oh_h,
                  dsend, drecv, fsend, frecv,
                  in_sem, k_sem, fs_sem, fr_sem, rs_sem, rr_sem, ds_sem, dr_sem, gs_sem, gr_sem):
@@ -318,21 +319,34 @@
         disp = [disp[c] + vel[c] for c in range(3)]
         return disp, vel
 
+    tiles = n // 8
+    mine = me // 8
+
+    def tile_at(k):
+        d = k // 4
+        step = lax.rem(2 + d + (d // 2) * (2 * d - 3), 4)
+        g = lax.rem(gx + 2 * step, nx)
+        g = g + (1 - 2 * lax.rem(g, 2)) * (1 - lax.rem(k // 2, 2))
+        half = lax.rem(yz // 8 + 1 - lax.rem(k, 2), 2)
+        return g, half
+
     send_disp(0, disp)
 
-    def fwd(a, b, g, y):
+    def fwd(g, y):
         return pltpu.make_async_remote_copy(
-            src_ref=s_ref.at[g * ny + y], dst_ref=recv.at[me], send_sem=fs_sem.at[a * ny + b], recv_sem=fr_sem.at[a * ny + b],
+            src_ref=s_ref.at[g * ny + y], dst_ref=recv.at[me], send_sem=fs_sem, recv_sem=fr_sem.at[mine],
             device_id=(g, y), device_id_type=MESH)
 
-    def fwd_start(b, _):
-        y = lax.rem(yz + b, ny)
-        for a in range(nx):
-            fwd(a, b, gx_at[a], y).start()
-        return 0
-    lax.fori_loop(1, ny, fwd_start, 0)
-    for a in range(1, nx):
-        fwd(a, 0, gx_at[a], yz).start()
+    def fwd_start(k, _):
+        g, half = tile_at(k)
+        for s in range(8):
+            y = half * 8 + lax.rem(yz + s, 8)
+
+            @pl.when(g * ny + y != me)
+            def _():
+                fwd(g, y).start()
+        return 0
+    lax.fori_loop(0, tiles, fwd_start, 0)
     recv[me] = s_ref[me]
     for dst in (con_lo, con_hi):
         dst[16:24, :] = jnp.zeros((8, 256), jnp.int32)
@@ -351,18 +365,22 @@
 
     sub128h = lax.broadcasted_iota(jnp.int32, (128, 128), 0).astype(jnp.int16)
 
-    tiles = n // 8
-    mine = me // 8
-
     def gather_load(k, acc):
-        base = pl.multiple_of(lax.rem(mine + tiles - k, tiles) * 8, 8)
-        a = lax.rem(gx + nx - base // ny, nx)
-        for s in range(8):
-            b = lax.rem(yz + ny - lax.rem(base, ny) - s, ny)
-
-            @pl.when(base + s != me)
-            def _():
-                fwd(a, b, gx, yz).wait_recv()
+        g, half = tile_at(k)
+        source = g * 2 + half
+        base = pl.multiple_of(source * 8, 8)
+        def arrive(count):
+            pltpu.make_async_remote_copy(
+                src_ref=s_ref.at[pl.ds(0, count)], dst_ref=recv.at[pl.ds(0, count)], send_sem=fs_sem, recv_sem=fr_sem.at[source],
+                device_id=(gx, yz), device_id_type=MESH).wait_recv()
+
+        @pl.when(source == mine)
+        def _():
+            arrive(7)
+
+        @pl.when(source != mine)
+        def _():
+            arrive(8)
         get = lambda r: recv[pl.ds(base, 8), r, :]
         loads = []
         for c in range(3):
@@ -400,12 +418,14 @@
             nd_ref[c:c + 1, 128 * h:128 * h + 128] = disp[c][h:h + 1, :]
             u_s[c, h:h + 1, 0:128] = disp[c][h:h + 1, :]
 
-    def ret(i):
-        t = lax.rem(me + i, n)
-        return near(outb.at[t], ret_ref.at[me], rs_sem.at[i], rr_sem.at[i], t)
+    def ret(g, y):
+        return pltpu.make_async_remote_copy(
+            src_ref=outb.at[g * ny + y], dst_ref=ret_ref.at[me], send_sem=rs_sem, recv_sem=rr_sem,
+            device_id=(g, y), device_id_type=MESH)
 
     def back(k, _):
-        base = pl.multiple_of(lax.rem(mine + k, tiles) * 8, 8)
+        g, half = tile_at(k)
+        base = pl.multiple_of((g * 2 + half) * 8, 8)
         sums = [[jnp.zeros((8, 128), F32)] * 4 for c in range(3)]
         for j in range(4):
             idx = ids[j, pl.ds(base, 8), :]
@@ -421,21 +441,23 @@
             outb[pl.ds(base, 8), 2 * c, :] = p0 + pltpu.roll(q0, 64, 1)
             outb[pl.ds(base, 8), 2 * c + 1, :] = p1 + pltpu.roll(q1, 64, 1)
         for s in range(8):
-            i = lax.rem(base + s + n - me, n)
-
-            @pl.when(i != 0)
+            y = half * 8 + lax.rem(yz + s, 8)
+
+            @pl.when(g * ny + y != me)
             def _():
-                ret(i).start()
+                ret(g, y).start()
         return 0
     lax.fori_loop(0, tiles, back, 0)
     ret_ref[me] = outb[me]
 
-    def drain(i, _):
-        fwd(i // ny, lax.rem(i, ny), gx, yz).wait_send()
-        ret(i).wait()
-        return 0
-    lax.fori_loop(1, n, drain, 0)
-    unpack_part(tgt_ref, slot_s, ret_ref, lhs, fd_ref)
+    def every(src, dst, ss, rs):
+        return pltpu.make_async_remote_copy(
+            src_ref=src.at[pl.ds(0, n - 1)], dst_ref=dst.at[pl.ds(0, n - 1)], send_sem=ss, recv_sem=rs,
+            device_id=(gx, yz), device_id_type=MESH)
+    every(s_ref, recv, fs_sem, fr_sem.at[0]).wait_send()
+    last = every(outb, ret_ref, rs_sem, rr_sem)
+    last.wait_send()
+    last.wait_recv()
 
 
 def solid(face_block, pressure, local, weight, area, nodes, target, stiffness, connect, halo, mass, disp, vel, nx, ny, shapes):
@@ -445,26 +467,35 @@
     D = pltpu.SemaphoreType.DMA
     M = pltpu.VMEM
     I32 = jnp.int32
-    return pl.pallas_call(
+    node_disp, back, slot = pl.pallas_call(
         functools.partial(solid_kernel, nx, ny, shapes),
-        out_shape=(jax.ShapeDtypeStruct(disp.shape, F32), jax.ShapeDtypeStruct((12, target.shape[1]), F32)),
+        out_shape=(jax.ShapeDtypeStruct(disp.shape, F32), jax.ShapeDtypeStruct((n, 6, 128), F32), jax.ShapeDtypeStruct(target.shape, I32)),
         in_specs=[pl.BlockSpec(memory_space=pltpu.SMEM), A, A, A, A, A, V, A, V, V, V, V, V],
-        out_specs=(V, V),
+        out_specs=(V, V, V),
         scratch_shapes=[
             M(pressure.shape, BF16), M(local.shape, I32), M(weight.shape, F32), M(area.shape, F32), M(nodes.shape, I32),
             M(area.shape, F32), M((16 * STRIDE, 128), F32), M((256, 32, 128), BF16), M((1024, 128), I32), M((1024, 128), F32),
-            M((1024, 128), F32), M(target.shape, I32), M((128, 256), F32), M((640, 256), F32),
-            M((n, 10, 128), F32), M((n, 6, 128), F32), M((768, 256), BF16),
+            M((1024, 128), F32), M((128, 256), F32), M((640, 256), F32),
+            M((n, 10, 128), F32),
             M((n, 10, 128), F32), M((n, 6, 128), F32), M((60, 60, 256), F32),
             M((4, n, 128), I32), M((24, 256), I32), M((24, 256), I32),
             M((3, 24, 256), F32), M((60, 256), F32), M((60, 256), F32),
             M((96, 5120), BF16), M((5120, 128), BF16), M((256, 128), BF16),
             M((SUBSTEPS, 2, 8, 128), F32), M((SUBSTEPS, 2, 8, 128), F32),
             M((SUBSTEPS, 2, 8, 128), F32), M((SUBSTEPS, 2, 8, 128), F32),
-            D((5,)), D, D((n,)), D((n,)), D((n,)), D((n,)), D((SUBSTEPS, 2)), D((SUBSTEPS, 2)), D((SUBSTEPS, 2)), D((SUBSTEPS, 2))],
+            D((5,)), D, D, D((n // 8,)), D, D, D((SUBSTEPS, 2)), D((SUBSTEPS, 2)), D((SUBSTEPS, 2)), D((SUBSTEPS, 2))],
         compiler_params=pltpu.CompilerParams(collective_id=0, has_side_effects=True, vmem_limit_bytes=56 * 2**20),
         name="solid",
     )(face_block, pressure, local, weight, area, nodes, target, stiffness, connect, halo, mass.reshape(1, -1), disp, vel)
+    return pl.pallas_call(
+        unpack_kernel,
+        out_shape=(jax.ShapeDtypeStruct(disp.shape, F32), jax.ShapeDtypeStruct((12, target.shape[1]), F32)),
+        in_specs=[V, V, V, V],
+        out_specs=(V, V),
+        scratch_shapes=[M((768, 256), BF16)],
+        compiler_params=pltpu.CompilerParams(vmem_limit_bytes=24 * 2**20),
+        name="unpack",
+    )(target, slot, back, node_disp)
 
 
 def shape_table():

time: 100 us -> 93.1 us (0.931)
  Pallas kernels: 96.4 us -> 89.6 us
    pallas_call x1, Pallas kernels: 96.4 us -> 85.5 us  [solid(): pl.pallas_call(functools.partial(solid_kernel, nx, ny, shapes), out_shape...]
    pallas_call x0 -> x1, Pallas kernels: none -> 4.07 us  [solid(): pl.pallas_call(unpack_kernel, out_shape=(jax.ShapeDtypeStruct(disp.shape,...]
    unnamed x2 -> x8, local copies, waits for them, and re-layouts: 3 us -> 2.47 us
where the time goes in v4:
time: 93.1 us; the launch traced here: 92.7 us
  Pallas kernels  89.6 us (96%)
  local copies, waits for them, and re-layouts  2.47 us (3%)
    pallas_call x1, Pallas kernels, solid(): pl.pallas_call(functools.partial(solid_kernel, nx, ny, shapes), out_shape...  85.5 us
    pallas_call x1, Pallas kernels, solid(): pl.pallas_call(unpack_kernel, out_shape=(jax.ShapeDtypeStruct(disp.shape,...  4.07 us
    unnamed x8, local copies, waits for them, and re-layouts  2.47 us

profile of v4, /device:TPU:1, one launch (start us, length us, event | category | flops | bytes accessed | tf_op | source)
XLA Modules:
  0.0 92.7 jit_solution(4718199946854988894)
XLA Ops:
  0.6 0.0 copy-start.1
  0.6 85.5 %solid.1 = (f32[3,1024]{1,0:T(4,128)}, f32[128,6,128]{2,1,0:T(8,128)}, s32[1,4096]{1,0:T(1,128)}) custom-call(s32[4096]{0:T(1024)} %fb_ref.1, bf16[256,4096]{1,0:T(8,128)(2,1)} %pr_hbm.1, s32[32,4096]{1,0:T(8,128)} %loc_hbm.1, f32[32,4096]{1,0:T(8,128)} %w_hbm.1, f32[12,4096]{1,0:T(8,128)} %an_hbm.1, s32[8,4096]{1,0:T(8,128)} %fn_hbm.1, s32[1,4096]{1,0:T(1,128)} %bitcast.2, ...), custom_call_target="tpu_custom_call" | custom-call | tf_op jit(solution)/shard_map/solid/pallas_call | solution.py:470
  86.2 0.0 copy-done.1
  86.2 0.0 copy-start
  86.2 1.0 %copy-done = f32[128,6,128]{2,1,0:T(8,128)S(1)} copy-done((f32[128,6,128]{2,1,0:T(8,128)S(1)}, f32[128,6,128]{2,1,0:T(8,128)}, u32[]{:S(2)}) %copy-start) | copy-done | bytes 393240
  87.2 0.0 copy-start.2
  87.2 0.7 copy-done.2
  88.0 0.0 copy-start.3
  88.0 0.7 copy-done.3
  88.7 4.1 %unpack.1 = (f32[3,1024]{1,0:T(4,128)}, f32[12,4096]{1,0:T(8,128)}) custom-call(s32[1,4096]{1,0:T(1,128)S(1)} %bitcast.3, s32[1,4096]{1,0:T(1,128)S(1)} %copy-done.3, f32[128,6,128]{2,1,0:T(8,128)S(1)} %copy-done, f32[3,1024]{1,0:T(4,128)S(1)} %copy-done.2), custom_call_target="tpu_custom_call" | custom-call | tf_op jit(solution)/shard_map/unpack/pallas_call | solution.py:490
Async XLA Ops:
  0.6 85.6 %copy-start.1 = (s32[4096,1]{0,1:T(1,128)S(1)}, s32[4096,1]{0,1:T(1,128)}, u32[]{:S(2)}) copy-start(s32[4096,1]{0,1:T(1,128)} %param.18) | copy-start | bytes 49156
  86.2 1.0 %copy-start = (f32[128,6,128]{2,1,0:T(8,128)S(1)}, f32[128,6,128]{2,1,0:T(8,128)}, u32[]{:S(2)}) copy-start(f32[128,6,128]{2,1,0:T(8,128)} %get-tuple-element.6.ret_ref) | copy-start | bytes 1179652
  87.2 0.7 copy-start.2
  88.0 0.7 copy-start.3

commit v5 on v4

--- a/solution.py
+++ b/solution.py
@@ -170,15 +170,13 @@
                  nd_ref, ret_ref, slot_s,
                  pr_ref, loc_ref, w_ref, an_ref, fn_ref, trac, tab32, tab, idxt, wt, res, carry, acc_s, s_ref,
                  recv, outb, kmat, ids, con_lo, con_hi, u_s, fh_s, fl_s, v_s, oh_e, oh_h,
-                 dsend, drecv, fsend, frecv,
-                 in_sem, k_sem, fs_sem, fr_sem, rs_sem, rr_sem, ds_sem, dr_sem, gs_sem, gr_sem):
+                 dsend, drecv, esend, erecv, fsend, frecv, ffar, eq_s,
+                 in_sem, k_sem, fs_sem, fr_sem, rs_sem, rr_sem, ds_sem, dr_sem, es_sem, er_sem, gs_sem, gr_sem, hs_sem, hr_sem):
     n = nx * ny
     gx = lax.axis_index("gx")
     yz = lax.axis_index("yz")
     me = gx * ny + yz
     dev = lambda t: (t // ny, lax.rem(t, ny))
-    nxt = lax.rem(me + 1, n)
-    prv = lax.rem(me + n - 1, n)
     ins = [pltpu.make_async_copy(src, dst, in_sem.at[k]) for k, (src, dst) in enumerate(
         ((loc_hbm, loc_ref), (w_hbm, w_ref), (pr_hbm, pr_ref), (an_hbm, an_ref), (fn_hbm, fn_ref)))]
     for cp in ins:
@@ -223,48 +221,79 @@
     def near(src, dst, ss, rs, t):
         return pltpu.make_async_remote_copy(src_ref=src, dst_ref=dst, send_sem=ss, recv_sem=rs, device_id=dev(t), device_id_type=MESH)
 
-    def disp_copies(step):
-        return [near(dsend.at[step, 1], drecv.at[step, 0], ds_sem.at[step, 1], dr_sem.at[step, 0], nxt),
-                near(dsend.at[step, 0], drecv.at[step, 1], ds_sem.at[step, 0], dr_sem.at[step, 1], prv)]
-
-    def force_copies(step):
-        return [near(fsend.at[step, 0], frecv.at[step, 1], gs_sem.at[step, 0], gr_sem.at[step, 1], prv),
-                near(fsend.at[step, 1], frecv.at[step, 0], gs_sem.at[step, 1], gr_sem.at[step, 0], nxt)]
+    def hop(send, recv, ss, rs, dist):
+        return (near(send(1), recv(0), ss(1), rs(0), lax.rem(me + dist, n)),
+                near(send(0), recv(1), ss(0), rs(1), lax.rem(me + n - dist, n)), dist)
 
     def start_both(copies):
-        up, down = copies
-
-        @pl.when(me < n - 1)
+        up, down, dist = copies
+
+        @pl.when(me < n - dist)
         def _():
             up.start()
 
-        @pl.when(me > 0)
+        @pl.when(me >= dist)
         def _():
             down.start()
 
     def wait_both(copies):
-        up, down = copies
-
-        @pl.when(me < n - 1)
+        up, down, dist = copies
+
+        @pl.when(me < n - dist)
         def _():
             up.wait_send()
             down.wait_recv()
 
-        @pl.when(me > 0)
+        @pl.when(me >= dist)
         def _():
             down.wait_send()
             up.wait_recv()
 
-    def send_disp(step, disp):
+    at = lambda ref, *lead: lambda side: ref.at[(*lead, side)]
+    state_copies = hop(at(dsend), at(drecv), at(ds_sem), at(dr_sem), 1)
+    load_copies = hop(at(esend), at(erecv), at(es_sem), at(er_sem), 1)
+    force_copies = lambda step: hop(at(fsend, step), at(frecv, step), at(gs_sem, step), at(gr_sem, step), 1)
+    far_copies = lambda step: hop(at(fsend, step), at(ffar, step), at(hs_sem, step), at(hr_sem, step), 2)
+    exists = [me > 0, me < n - 1]
+    exists_far = [me > 1, me < n - 2]
+
+    def pick(r, x):
+        g = jnp.where(halo_hi[r] == sub8, lane_take(x, halo_lo[r]), F32(0))
+        return jnp.sum(g, axis=0, keepdims=True)
+
+    def send_state():
         for r in range(2):
             for c in range(3):
-                g = jnp.where(halo_hi[r] == sub8, lane_take(disp[c], halo_lo[r]), F32(0))
-                dsend[step, r, c:c + 1, :] = jnp.sum(g, axis=0, keepdims=True)
-        start_both(disp_copies(step))
-
-    def internal(step, disp):
-        wait_both(disp_copies(step))
-        ghost = [jnp.where(me > 0, drecv[step, 0, 0:3, :], F32(0)), jnp.where(me < n - 1, drecv[step, 1, 0:3, :], F32(0))]
+                dsend[r, c:c + 1, :] = pick(r, disp[c])
+                dsend[r, 3 + c:4 + c, :] = pick(r, vel[c])
+            dsend[r, 6:7, :] = pick(r, mass)
+            dsend[r, 8:10, :] = halo_ref[...].astype(F32)
+        start_both(state_copies)
+
+    def ghost_state():
+        wait_both(state_copies)
+        gd = [jnp.where(exists[k], drecv[k, 0:3, :], F32(0)) for k in range(2)]
+        gv = [jnp.where(exists[k], drecv[k, 3:6, :], F32(0)) for k in range(2)]
+        gm = [jnp.where(exists[k], drecv[k, 6:7, :], F32(1)) for k in range(2)]
+        for k in range(2):
+            held, other = drecv[k, 9 - k:10 - k, :], drecv[k, 8 + k:9 + k, :]
+            for m, x in enumerate((held, other)):
+                same = jnp.broadcast_to(x, (128, 128)).T == jnp.broadcast_to(held, (128, 128))
+                eq_s[k, 128 * m:128 * m + 128, :] = jnp.where(same, F32(1), F32(0)).astype(BF16)
+        return gd, gv, gm
+
+    def advance_ghosts(step, ge, gd, gv, gm):
+        wait_both(far_copies(step))
+        for k in range(2):
+            x = jnp.concatenate([fsend[step, k], jnp.where(exists_far[k], ffar[step, k], F32(0))], axis=1)
+            xh = x.astype(BF16).astype(F32)
+            both = jnp.dot(jnp.concatenate([xh, x - xh], axis=0).astype(BF16), eq_s[k], preferred_element_type=F32)
+            total = frecv[step, k, 3:6, :] + (both[0:3] + both[8:11])
+            v = gv[k] + (ge[k] - total) / gm[k]
+            gv[k] = jnp.where(exists[k], v, F32(0))
+            gd[k] = gd[k] + gv[k]
+
+    def internal(step, disp, ghost):
         for c in range(3):
             rows = [disp[c][h:h + 1, :] for h in range(8)] + [ghost[0][c:c + 1, :], ghost[1][c:c + 1, :]]
             rows = [jnp.broadcast_to(r, (8, 128)) for r in rows]
@@ -294,14 +323,19 @@
                     v_s[48 * k + 16 * c:48 * k + 16 * c + 16, a * 256:a * 256 + 256] = jnp.where(mask, row, F32(0)).astype(BF16)
         both = jnp.dot(v_s[...], oh_e[...], preferred_element_type=F32)
         total = both[:48] + both[48:]
+        own = [total[16 * c:16 * c + 8, :] for c in range(3)]
         for k in range(2):
             for c in range(3):
                 fsend[step, k, c:c + 1, :] = total[16 * c + 8 + k:16 * c + 9 + k, :]
-        start_both(force_copies(step)[::-1])
-        return [total[16 * c:16 * c + 8, :] for c in range(3)]
+                fsend[step, k, 3 + c:4 + c, :] = pick(k, own[c])
+            fsend[step, k, 6:8, :] = jnp.zeros((2, 128), F32)
+        start_both(force_copies(step))
+        if step < SUBSTEPS - 1:
+            start_both(far_copies(step))
+        return own
 
     def advance(step, own, ext, disp, vel):
-        wait_both(force_copies(step)[::-1])
+        wait_both(force_copies(step))
         got = [jnp.where(me > 0, frecv[step, 0, 0:3, :], F32(0)), jnp.where(me < n - 1, frecv[step, 1, 0:3, :], F32(0))]
         parts = []
         for c in range(3):
@@ -330,7 +364,7 @@
         half = lax.rem(yz // 8 + 1 - lax.rem(k, 2), 2)
         return g, half
 
-    send_disp(0, disp)
+    send_state()
 
     def fwd(g, y):
         return pltpu.make_async_remote_copy(
@@ -360,7 +394,8 @@
         row = jnp.broadcast_to(halo_ref[r:r + 1, :] & 127, (128, 128))
         oh_h[128 * r:128 * r + 128, :] = jnp.where(row == sub128, F32(1), F32(0)).T.astype(BF16)
     kcopy.wait()
-    own = internal(0, disp)
+    gd, gv, gm = ghost_state()
+    own = internal(0, disp, gd)
 
 
     sub128h = lax.broadcasted_iota(jnp.int32, (128, 128), 0).astype(jnp.int16)
@@ -408,11 +443,20 @@
     both = lax.fori_loop(0, tiles, gather_load, jnp.zeros((48, 128), F32))
     ext = [both[8 * c:8 * c + 8] + both[24 + 8 * c:32 + 8 * c] for c in range(3)]
 
+    for r in range(2):
+        for c in range(3):
+            esend[r, c:c + 1, :] = pick(r, ext[c])
+        esend[r, 3:8, :] = jnp.zeros((5, 128), F32)
+    start_both(load_copies)
     disp, vel = advance(0, own, ext, disp, vel)
+    wait_both(load_copies)
+    ge = [jnp.where(exists[k], erecv[k, 0:3, :], F32(0)) for k in range(2)]
+    advance_ghosts(0, ge, gd, gv, gm)
     for step in range(1, SUBSTEPS):
-        send_disp(step, disp)
-        own = internal(step, disp)
+        own = internal(step, disp, gd)
         disp, vel = advance(step, own, ext, disp, vel)
+        if step < SUBSTEPS - 1:
+            advance_ghosts(step, ge, gd, gv, gm)
     for c in range(3):
         for h in range(8):
             nd_ref[c:c + 1, 128 * h:128 * h + 128] = disp[c][h:h + 1, :]
@@ -481,9 +525,10 @@
             M((4, n, 128), I32), M((24, 256), I32), M((24, 256), I32),
             M((3, 24, 256), F32), M((60, 256), F32), M((60, 256), F32),
             M((96, 5120), BF16), M((5120, 128), BF16), M((256, 128), BF16),
-            M((SUBSTEPS, 2, 8, 128), F32), M((SUBSTEPS, 2, 8, 128), F32),
-            M((SUBSTEPS, 2, 8, 128), F32), M((SUBSTEPS, 2, 8, 128), F32),
-            D((5,)), D, D, D((n // 8,)), D, D, D((SUBSTEPS, 2)), D((SUBSTEPS, 2)), D((SUBSTEPS, 2)), D((SUBSTEPS, 2))],
+            M((2, 16, 128), F32), M((2, 16, 128), F32), M((2, 8, 128), F32), M((2, 8, 128), F32),
+            M((SUBSTEPS, 2, 8, 128), F32), M((SUBSTEPS, 2, 8, 128), F32), M((SUBSTEPS, 2, 8, 128), F32), M((2, 256, 128), BF16),
+            D((5,)), D, D, D((n // 8,)), D, D, D((2,)), D((2,)), D((2,)), D((2,)),
+            D((SUBSTEPS, 2)), D((SUBSTEPS, 2)), D((SUBSTEPS, 2)), D((SUBSTEPS, 2))],
         compiler_params=pltpu.CompilerParams(collective_id=0, has_side_effects=True, vmem_limit_bytes=56 * 2**20),
         name="solid",
     )(face_block, pressure, local, weight, area, nodes, target, stiffness, connect, halo, mass.reshape(1, -1), disp, vel)

time: 93.1 us -> 85 us (0.913)
  Pallas kernels: 89.6 us -> 81.5 us
    pallas_call x1, Pallas kernels: 85.5 us -> 77.4 us  [solid(): pl.pallas_call(functools.partial(solid_kernel, nx, ny, shapes), out_shape...]
where the time goes in v5:
time: 85 us; the launch traced here: 84.6 us
  Pallas kernels  81.5 us (96%)
  local copies, waits for them, and re-layouts  2.47 us (3%)
    pallas_call x1, Pallas kernels, solid(): pl.pallas_call(functools.partial(solid_kernel, nx, ny, shapes), out_shape...  77.4 us
    pallas_call x1, Pallas kernels, solid(): pl.pallas_call(unpack_kernel, out_shape=(jax.ShapeDtypeStruct(disp.shape,...  4.07 us
    unnamed x8, local copies, waits for them, and re-layouts  2.47 us

profile of v5, /device:TPU:1, one launch (start us, length us, event | category | flops | bytes accessed | tf_op | source)
XLA Modules:
  0.0 84.6 jit_solution(6374795619712481779)
XLA Ops:
  0.6 0.0 copy-start.1
  0.6 77.4 %solid.1 = (f32[3,1024]{1,0:T(4,128)}, f32[128,6,128]{2,1,0:T(8,128)}, s32[1,4096]{1,0:T(1,128)}) custom-call(s32[4096]{0:T(1024)} %fb_ref.1, bf16[256,4096]{1,0:T(8,128)(2,1)} %pr_hbm.1, s32[32,4096]{1,0:T(8,128)} %loc_hbm.1, f32[32,4096]{1,0:T(8,128)} %w_hbm.1, f32[12,4096]{1,0:T(8,128)} %an_hbm.1, s32[8,4096]{1,0:T(8,128)} %fn_hbm.1, s32[1,4096]{1,0:T(1,128)} %bitcast.2, ...), custom_call_target="tpu_custom_call" | custom-call | tf_op jit(solution)/shard_map/solid/pallas_call | solution.py:514
  78.1 0.0 copy-done.1
  78.1 0.0 copy-start
  78.1 1.0 %copy-done = f32[128,6,128]{2,1,0:T(8,128)S(1)} copy-done((f32[128,6,128]{2,1,0:T(8,128)S(1)}, f32[128,6,128]{2,1,0:T(8,128)}, u32[]{:S(2)}) %copy-start) | copy-done | bytes 393240
  79.1 0.0 copy-start.2
  79.1 0.7 copy-done.2
  79.8 0.0 copy-start.3
  79.8 0.7 copy-done.3
  80.6 4.1 %unpack.1 = (f32[3,1024]{1,0:T(4,128)}, f32[12,4096]{1,0:T(8,128)}) custom-call(s32[1,4096]{1,0:T(1,128)S(1)} %bitcast.3, s32[1,4096]{1,0:T(1,128)S(1)} %copy-done.3, f32[128,6,128]{2,1,0:T(8,128)S(1)} %copy-done, f32[3,1024]{1,0:T(4,128)S(1)} %copy-done.2), custom_call_target="tpu_custom_call" | custom-call | tf_op jit(solution)/shard_map/unpack/pallas_call | solution.py:535
Async XLA Ops:
  0.6 77.4 %copy-start.1 = (s32[4096,1]{0,1:T(1,128)S(1)}, s32[4096,1]{0,1:T(1,128)}, u32[]{:S(2)}) copy-start(s32[4096,1]{0,1:T(1,128)} %param.18) | copy-start | bytes 49156
  78.1 1.0 %copy-start = (f32[128,6,128]{2,1,0:T(8,128)S(1)}, f32[128,6,128]{2,1,0:T(8,128)}, u32[]{:S(2)}) copy-start(f32[128,6,128]{2,1,0:T(8,128)} %get-tuple-element.6.ret_ref) | copy-start | bytes 1179652
  79.1 0.7 copy-start.2
  79.8 0.7 copy-start.3

commit v6 on v5

--- a/solution.py
+++ b/solution.py
@@ -29,7 +29,7 @@
     return out
 
 STRIDE = 40
-UNR = 32
+UNR = 64
 TAKE = lax.GatherDimensionNumbers(
     offset_dims=(), collapsed_slice_dims=(1,), start_index_map=(1,), operand_batching_dims=(0,), start_indices_batching_dims=(0,)
 )
@@ -144,13 +144,19 @@
         send_ref[:, r, :] = jnp.concatenate(block, axis=0).T
 
 
-def unpack_kernel(tgt_ref, slot_s, ret_ref, nd_in, nd_ref, fd_ref, lhs):
-    nd_ref[...] = nd_in[...]
+def unpack_kernel(n, tgt_ref, ret_ref, nd_ref, fd_ref, slot_s, lhs):
+    for r in range(56):
+        row = ret_ref[n + r // 6, r % 6:r % 6 + 1, :]
+        if r < 32:
+            slot_s[:, 128 * r:128 * r + 128] = row.astype(jnp.int32)
+        else:
+            c, h = divmod(r - 32, 8)
+            nd_ref[c:c + 1, 128 * h:128 * h + 128] = row
     wide = 512
     rows128 = lax.broadcasted_iota(jnp.int32, (128, wide), 0)
     rows64 = lax.broadcasted_iota(jnp.int32, (64, wide), 0)
     for r in range(6):
-        x = ret_ref[:, r, :].T
+        x = ret_ref[0:n, r, :].T
         xh = x.astype(BF16).astype(F32)
         lhs[128 * r:128 * r + 128, :] = jnp.concatenate([xh, x - xh], axis=1).astype(BF16)
 
@@ -167,8 +173,8 @@
 
 
 def solid_kernel(nx, ny, shapes, fb_ref, pr_hbm, loc_hbm, w_hbm, an_hbm, fn_hbm, tgt_ref, k_hbm, con_ref, halo_ref, mass_ref, disp_ref, vel_ref,
-                 nd_ref, ret_ref, slot_s,
-                 pr_ref, loc_ref, w_ref, an_ref, fn_ref, trac, tab32, tab, idxt, wt, res, carry, acc_s, s_ref,
+                 ret_ref,
+                 pr_ref, loc_ref, w_ref, an_ref, fn_ref, trac, tab32, tab, idxt, wt, res, slot_s, carry, acc_s, s_ref,
                  recv, outb, kmat, ids, con_lo, con_hi, u_s, fh_s, fl_s, v_s, oh_e, oh_h,
                  dsend, drecv, esend, erecv, fsend, frecv, ffar, eq_s,
                  in_sem, k_sem, fs_sem, fr_sem, rs_sem, rr_sem, ds_sem, dr_sem, es_sem, er_sem, gs_sem, gr_sem, hs_sem, hr_sem):
@@ -459,8 +465,11 @@
             advance_ghosts(step, ge, gd, gv, gm)
     for c in range(3):
         for h in range(8):
-            nd_ref[c:c + 1, 128 * h:128 * h + 128] = disp[c][h:h + 1, :]
+            at_row = 32 + 8 * c + h
+            ret_ref[n + at_row // 6, at_row % 6:at_row % 6 + 1, :] = disp[c][h:h + 1, :]
             u_s[c, h:h + 1, 0:128] = disp[c][h:h + 1, :]
+    for r in range(32):
+        ret_ref[n + r // 6, r % 6:r % 6 + 1, :] = slot_s[:, 128 * r:128 * r + 128].astype(F32)
 
     def ret(g, y):
         return pltpu.make_async_remote_copy(
@@ -468,30 +477,32 @@
             device_id=(g, y), device_id_type=MESH)
 
     def back(k, _):
-        g, half = tile_at(k)
-        base = pl.multiple_of((g * 2 + half) * 8, 8)
-        sums = [[jnp.zeros((8, 128), F32)] * 4 for c in range(3)]
-        for j in range(4):
-            idx = ids[j, pl.ds(base, 8), :]
-            lo, hi = idx & 127, idx >> 7
-            masks = [hi == h for h in range(1, 8)]
+        pair = [tile_at(2 * k + m) for m in range(2)]
+        for g, half in pair:
+            base = pl.multiple_of((g * 2 + half) * 8, 8)
+            sums = [[jnp.zeros((8, 128), F32)] * 4 for c in range(3)]
+            for j in range(4):
+                idx = ids[j, pl.ds(base, 8), :]
+                lo, hi = idx & 127, idx >> 7
+                masks = [hi == h for h in range(1, 8)]
+                for c in range(3):
+                    acc = lane_take(jnp.broadcast_to(u_s[c, 0:1, 0:128], (8, 128)), lo)
+                    for h in range(1, 8):
+                        acc = jnp.where(masks[h - 1], lane_take(jnp.broadcast_to(u_s[c, h:h + 1, 0:128], (8, 128)), lo), acc)
+                    sums[c] = [sums[c][m] + weights[j][m] * acc for m in range(4)]
             for c in range(3):
-                acc = lane_take(jnp.broadcast_to(u_s[c, 0:1, 0:128], (8, 128)), lo)
-                for h in range(1, 8):
-                    acc = jnp.where(masks[h - 1], lane_take(jnp.broadcast_to(u_s[c, h:h + 1, 0:128], (8, 128)), lo), acc)
-                sums[c] = [sums[c][m] + weights[j][m] * acc for m in range(4)]
-        for c in range(3):
-            p0, q0, p1, q1 = sums[c]
-            outb[pl.ds(base, 8), 2 * c, :] = p0 + pltpu.roll(q0, 64, 1)
-            outb[pl.ds(base, 8), 2 * c + 1, :] = p1 + pltpu.roll(q1, 64, 1)
-        for s in range(8):
-            y = half * 8 + lax.rem(yz + s, 8)
-
-            @pl.when(g * ny + y != me)
-            def _():
-                ret(g, y).start()
-        return 0
-    lax.fori_loop(0, tiles, back, 0)
+                p0, q0, p1, q1 = sums[c]
+                outb[pl.ds(base, 8), 2 * c, :] = p0 + pltpu.roll(q0, 64, 1)
+                outb[pl.ds(base, 8), 2 * c + 1, :] = p1 + pltpu.roll(q1, 64, 1)
+        for g, half in pair:
+            for s in range(8):
+                y = half * 8 + lax.rem(yz + s, 8)
+
+                @pl.when(g * ny + y != me)
+                def _():
+                    ret(g, y).start()
+        return 0
+    lax.fori_loop(0, tiles // 2, back, 0)
     ret_ref[me] = outb[me]
 
     def every(src, dst, ss, rs):
@@ -511,15 +522,15 @@
     D = pltpu.SemaphoreType.DMA
     M = pltpu.VMEM
     I32 = jnp.int32
-    node_disp, back, slot = pl.pallas_call(
+    back = pl.pallas_call(
         functools.partial(solid_kernel, nx, ny, shapes),
-        out_shape=(jax.ShapeDtypeStruct(disp.shape, F32), jax.ShapeDtypeStruct((n, 6, 128), F32), jax.ShapeDtypeStruct(target.shape, I32)),
+        out_shape=jax.ShapeDtypeStruct((n + 10, 6, 128), F32),
         in_specs=[pl.BlockSpec(memory_space=pltpu.SMEM), A, A, A, A, A, V, A, V, V, V, V, V],
-        out_specs=(V, V, V),
+        out_specs=V,
         scratch_shapes=[
             M(pressure.shape, BF16), M(local.shape, I32), M(weight.shape, F32), M(area.shape, F32), M(nodes.shape, I32),
             M(area.shape, F32), M((16 * STRIDE, 128), F32), M((256, 32, 128), BF16), M((1024, 128), I32), M((1024, 128), F32),
-            M((1024, 128), F32), M((128, 256), F32), M((640, 256), F32),
+            M((1024, 128), F32), M(target.shape, I32), M((128, 256), F32), M((640, 256), F32),
             M((n, 10, 128), F32),
             M((n, 10, 128), F32), M((n, 6, 128), F32), M((60, 60, 256), F32),
             M((4, n, 128), I32), M((24, 256), I32), M((24, 256), I32),
@@ -533,14 +544,14 @@
         name="solid",
     )(face_block, pressure, local, weight, area, nodes, target, stiffness, connect, halo, mass.reshape(1, -1), disp, vel)
     return pl.pallas_call(
-        unpack_kernel,
+        functools.partial(unpack_kernel, n),
         out_shape=(jax.ShapeDtypeStruct(disp.shape, F32), jax.ShapeDtypeStruct((12, target.shape[1]), F32)),
-        in_specs=[V, V, V, V],
+        in_specs=[V, V],
         out_specs=(V, V),
-        scratch_shapes=[M((768, 256), BF16)],
+        scratch_shapes=[M(target.shape, I32), M((768, 256), BF16)],
         compiler_params=pltpu.CompilerParams(vmem_limit_bytes=24 * 2**20),
         name="unpack",
-    )(target, slot, back, node_disp)
+    )(target, back)
 
 
 def shape_table():

time: 85 us -> 81.5 us (0.959)
  Pallas kernels: 81.5 us -> 79.5 us
  local copies, waits for them, and re-layouts: 2.47 us -> 1.05 us
    pallas_call x1, Pallas kernels: 77.4 us -> 75.4 us  [solid(): pl.pallas_call(functools.partial(solid_kernel, nx, ny, shapes), out_shape...]
    unnamed x8 -> x4, local copies, waits for them, and re-layouts: 2.47 us -> 1.05 us
where the time goes in v6:
time: 81.5 us; the launch traced here: 81.2 us
  Pallas kernels  79.5 us (98%)
  local copies, waits for them, and re-layouts  1.05 us (1%)
    pallas_call x1, Pallas kernels, solid(): pl.pallas_call(functools.partial(solid_kernel, nx, ny, shapes), out_shape...  75.4 us
    pallas_call x1, Pallas kernels, solid(): pl.pallas_call(functools.partial(unpack_kernel, n), out_shape=(jax.ShapeD...  4.06 us

profile of v6, /device:TPU:1, one launch (start us, length us, event | category | flops | bytes accessed | tf_op | source)
XLA Modules:
  0.0 81.2 jit_solution(4420833478157189939)
XLA Ops:
  0.6 0.0 copy-start.1
  0.6 75.4 %solid.1.ret_ref = f32[138,6,128]{2,1,0:T(8,128)} custom-call(s32[4096]{0:T(1024)} %fb_ref.1, bf16[256,4096]{1,0:T(8,128)(2,1)} %pr_hbm.1, s32[32,4096]{1,0:T(8,128)} %loc_hbm.1, f32[32,4096]{1,0:T(8,128)} %w_hbm.1, f32[12,4096]{1,0:T(8,128)} %an_hbm.1, s32[8,4096]{1,0:T(8,128)} %fn_hbm.1, s32[1,4096]{1,0:T(1,128)} %bitcast.2, f32[60,60,256]{2,1,0:T(8,128)} %k_hbm.1, ...), custom_call_target="tpu_custom_call" | custom-call | tf_op jit(solution)/shard_map/solid/pallas_call | solution.py:525
  76.1 0.0 copy-done.1
  76.1 0.0 copy-start
  76.1 1.0 %copy-done = f32[138,6,128]{2,1,0:T(8,128)S(1)} copy-done((f32[138,6,128]{2,1,0:T(8,128)S(1)}, f32[138,6,128]{2,1,0:T(8,128)}, u32[]{:S(2)}) %copy-start) | copy-done | bytes 423960
  77.2 4.1 %unpack.1 = (f32[3,1024]{1,0:T(4,128)}, f32[12,4096]{1,0:T(8,128)}) custom-call(s32[1,4096]{1,0:T(1,128)S(1)} %bitcast.3, f32[138,6,128]{2,1,0:T(8,128)S(1)} %copy-done), custom_call_target="tpu_custom_call" | custom-call | tf_op jit(solution)/shard_map/unpack/pallas_call | solution.py:546
Async XLA Ops:
  0.6 75.5 %copy-start.1 = (s32[4096,1]{0,1:T(1,128)S(1)}, s32[4096,1]{0,1:T(1,128)}, u32[]{:S(2)}) copy-start(s32[4096,1]{0,1:T(1,128)} %param.18) | copy-start | bytes 49156
  76.1 1.1 %copy-start = (f32[138,6,128]{2,1,0:T(8,128)S(1)}, f32[138,6,128]{2,1,0:T(8,128)}, u32[]{:S(2)}) copy-start(f32[138,6,128]{2,1,0:T(8,128)} %solid.1.ret_ref) | copy-start | bytes 1271812

commit v7 on v6

--- a/solution.py
+++ b/solution.py
@@ -29,7 +29,7 @@
     return out
 
 STRIDE = 40
-UNR = 64
+UNR = 128
 TAKE = lax.GatherDimensionNumbers(
     offset_dims=(), collapsed_slice_dims=(1,), start_index_map=(1,), operand_batching_dims=(0,), start_indices_batching_dims=(0,)
 )
@@ -94,7 +94,7 @@
 
 
 def pack_part(tgt_ref, fn_ref, trac, slot_s, carry, acc, send_ref):
-    wide = 1024
+    wide = 2048
     rows128 = lax.broadcasted_iota(jnp.int32, (128, 256), 0)
     rows256 = lax.broadcasted_iota(jnp.int32, (256, 256), 0)
     cols256 = lax.broadcasted_iota(jnp.int32, (256, 256), 1)
@@ -108,7 +108,7 @@
 
     def rank(kt, _):
         before = carry[...]
-        for m in range(4):
+        for m in range(8):
             at = pl.ds(pl.multiple_of(kt * wide + 256 * m, 256), 256)
             hit = jnp.broadcast_to(tgt_ref[:, at], (128, 256)) == rows128
             hot = one_if(hit)
@@ -117,7 +117,7 @@
             before = before + jnp.dot(hot, ones, preferred_element_type=F32)
         carry[...] = before
         return 0
-    lax.fori_loop(0, 4, rank, 0)
+    lax.fori_loop(0, 2, rank, 0)
 
     def tile(kt, _):
         at = pl.ds(pl.multiple_of(kt * wide, wide), wide)
@@ -138,7 +138,7 @@
             total = y if total is None else total + y
         acc[...] += total
         return 0
-    lax.fori_loop(0, 4, tile, 0)
+    lax.fori_loop(0, 2, tile, 0)
     for r in range(10):
         block = [acc[32 * v:32 * v + 32, 128 * h:128 * h + 128] for v in (2 * r, 2 * r + 1) for h in range(2)]
         send_ref[:, r, :] = jnp.concatenate(block, axis=0).T
@@ -152,7 +152,7 @@
         else:
             c, h = divmod(r - 32, 8)
             nd_ref[c:c + 1, 128 * h:128 * h + 128] = row
-    wide = 512
+    wide = 1024
     rows128 = lax.broadcasted_iota(jnp.int32, (128, wide), 0)
     rows64 = lax.broadcasted_iota(jnp.int32, (64, wide), 0)
     for r in range(6):
@@ -169,7 +169,7 @@
             [jnp.sum(jnp.where(mask, y[64 * v:64 * v + 64, :], F32(0)), axis=0, keepdims=True) for v in range(12)], axis=0
         )
         return 0
-    lax.fori_loop(0, 8, tile, 0)
+    lax.fori_loop(0, 4, tile, 0)
 
 
 def solid_kernel(nx, ny, shapes, fb_ref, pr_hbm, loc_hbm, w_hbm, an_hbm, fn_hbm, tgt_ref, k_hbm, con_ref, halo_ref, mass_ref, disp_ref, vel_ref,
@@ -362,6 +362,9 @@
     tiles = n // 8
     mine = me // 8
 
+    spread = [lax.rem(yz + s, 8) for s in range(8)]
+    own_half = yz // 8
+
     def tile_at(k):
         d = k // 4
         step = lax.rem(2 + d + (d // 2) * (2 * d - 3), 4)
@@ -380,13 +383,11 @@
     def fwd_start(k, _):
         g, half = tile_at(k)
         for s in range(8):
-            y = half * 8 + lax.rem(yz + s, 8)
-
-            @pl.when(g * ny + y != me)
-            def _():
-                fwd(g, y).start()
-        return 0
-    lax.fori_loop(0, tiles, fwd_start, 0)
+            fwd(g, half * 8 + spread[s]).start()
+        return 0
+    lax.fori_loop(0, tiles - 1, fwd_start, 0)
+    for s in range(1, 8):
+        fwd(gx, own_half * 8 + spread[s]).start()
     recv[me] = s_ref[me]
     for dst in (con_lo, con_hi):
         dst[16:24, :] = jnp.zeros((8, 256), jnp.int32)
@@ -406,22 +407,13 @@
 
     sub128h = lax.broadcasted_iota(jnp.int32, (128, 128), 0).astype(jnp.int16)
 
-    def gather_load(k, acc):
-        g, half = tile_at(k)
-        source = g * 2 + half
+    def arrive(source, count):
+        pltpu.make_async_remote_copy(
+            src_ref=s_ref.at[pl.ds(0, count)], dst_ref=recv.at[pl.ds(0, count)], send_sem=fs_sem, recv_sem=fr_sem.at[source],
+            device_id=(gx, yz), device_id_type=MESH).wait_recv()
+
+    def load_of(source, acc):
         base = pl.multiple_of(source * 8, 8)
-        def arrive(count):
-            pltpu.make_async_remote_copy(
-                src_ref=s_ref.at[pl.ds(0, count)], dst_ref=recv.at[pl.ds(0, count)], send_sem=fs_sem, recv_sem=fr_sem.at[source],
-                device_id=(gx, yz), device_id_type=MESH).wait_recv()
-
-        @pl.when(source == mine)
-        def _():
-            arrive(7)
-
-        @pl.when(source != mine)
-        def _():
-            arrive(8)
         get = lambda r: recv[pl.ds(base, 8), r, :]
         loads = []
         for c in range(3):
@@ -446,7 +438,19 @@
                 total = total + lax.dot_general(
                     jnp.concatenate(vals, axis=1), jnp.concatenate(hots, axis=1), (((1,), (1,)), ((), ())), preferred_element_type=F32)
         return acc + total
-    both = lax.fori_loop(0, tiles, gather_load, jnp.zeros((48, 128), F32))
+    def gather_load(k, acc):
+        sources = []
+        for m in range(3):
+            g, half = tile_at(3 * k + m)
+            sources.append(g * 2 + half)
+            arrive(sources[m], 8)
+        for source in sources:
+            acc = load_of(source, acc)
+        return acc
+
+    both = lax.fori_loop(0, (tiles - 1) // 3, gather_load, jnp.zeros((48, 128), F32))
+    arrive(mine, 7)
+    both = load_of(mine, both)
     ext = [both[8 * c:8 * c + 8] + both[24 + 8 * c:32 + 8 * c] for c in range(3)]
 
     for r in range(2):

time: 81.5 us -> 78.9 us (0.968)
  Pallas kernels: 79.5 us -> 76.9 us
    pallas_call x1, Pallas kernels: 75.4 us -> 73.5 us  [solid(): pl.pallas_call(functools.partial(solid_kernel, nx, ny, shapes), out_shape...]
where the time goes in v7:
time: 78.9 us; the launch traced here: 78.7 us
  Pallas kernels  76.9 us (97%)
  local copies, waits for them, and re-layouts  1.05 us (1%)
    pallas_call x1, Pallas kernels, solid(): pl.pallas_call(functools.partial(solid_kernel, nx, ny, shapes), out_shape...  73.5 us
    pallas_call x1, Pallas kernels, solid(): pl.pallas_call(functools.partial(unpack_kernel, n), out_shape=(jax.ShapeD...  3.44 us

profile of v7, /device:TPU:1, one launch (start us, length us, event | category | flops | bytes accessed | tf_op | source)
XLA Modules:
  0.0 78.7 jit_solution(9279994339619275313)
XLA Ops:
  0.6 0.0 copy-start.1
  0.6 73.5 %solid.1.ret_ref = f32[138,6,128]{2,1,0:T(8,128)} custom-call(s32[4096]{0:T(1024)} %fb_ref.1, bf16[256,4096]{1,0:T(8,128)(2,1)} %pr_hbm.1, s32[32,4096]{1,0:T(8,128)} %loc_hbm.1, f32[32,4096]{1,0:T(8,128)} %w_hbm.1, f32[12,4096]{1,0:T(8,128)} %an_hbm.1, s32[8,4096]{1,0:T(8,128)} %fn_hbm.1, s32[1,4096]{1,0:T(1,128)} %bitcast.2, f32[60,60,256]{2,1,0:T(8,128)} %k_hbm.1, ...), custom_call_target="tpu_custom_call" | custom-call | tf_op jit(solution)/shard_map/solid/pallas_call | solution.py:529
  74.2 0.0 copy-done.1
  74.2 0.0 copy-start
  74.2 1.0 %copy-done = f32[138,6,128]{2,1,0:T(8,128)S(1)} copy-done((f32[138,6,128]{2,1,0:T(8,128)S(1)}, f32[138,6,128]{2,1,0:T(8,128)}, u32[]{:S(2)}) %copy-start) | copy-done | bytes 423960
  75.2 3.4 %unpack.1 = (f32[3,1024]{1,0:T(4,128)}, f32[12,4096]{1,0:T(8,128)}) custom-call(s32[1,4096]{1,0:T(1,128)S(1)} %bitcast.3, f32[138,6,128]{2,1,0:T(8,128)S(1)} %copy-done), custom_call_target="tpu_custom_call" | custom-call | tf_op jit(solution)/shard_map/unpack/pallas_call | solution.py:550
Async XLA Ops:
  0.6 73.5 %copy-start.1 = (s32[4096,1]{0,1:T(1,128)S(1)}, s32[4096,1]{0,1:T(1,128)}, u32[]{:S(2)}) copy-start(s32[4096,1]{0,1:T(1,128)} %param.18) | copy-start | bytes 49156
  74.2 1.1 %copy-start = (f32[138,6,128]{2,1,0:T(8,128)S(1)}, f32[138,6,128]{2,1,0:T(8,128)}, u32[]{:S(2)}) copy-start(f32[138,6,128]{2,1,0:T(8,128)} %solid.1.ret_ref) | copy-start | bytes 1271812

commit v8 on v7

--- a/solution.py
+++ b/solution.py
@@ -93,18 +93,15 @@
             out_ref[:, f0:f0 + 128] = -(an_ref[:, f0:f0 + 128] * fp3)
 
 
-def pack_part(tgt_ref, fn_ref, trac, slot_s, carry, acc, send_ref):
+def rank_part(tgt_ref, slot_s, carry):
     wide = 2048
     rows128 = lax.broadcasted_iota(jnp.int32, (128, 256), 0)
     rows256 = lax.broadcasted_iota(jnp.int32, (256, 256), 0)
     cols256 = lax.broadcasted_iota(jnp.int32, (256, 256), 1)
-    rows256w = lax.broadcasted_iota(jnp.int32, (256, wide), 0)
-    rows32 = lax.broadcasted_iota(jnp.int32, (32, wide), 0)
     one_if = lambda m: jnp.where(m, F32(1), F32(0)).astype(BF16)
     upper = one_if(rows256 < cols256)
     ones = jnp.ones((256, 256), BF16)
     carry[...] = jnp.zeros_like(carry)
-    acc[...] = jnp.zeros_like(acc)
 
     def rank(kt, _):
         before = carry[...]
@@ -118,6 +115,17 @@
         carry[...] = before
         return 0
     lax.fori_loop(0, 2, rank, 0)
+
+
+def pack_part(tgt_ref, fn_ref, trac, slot_s, acc, send_ref):
+    wide = 2048
+    rows128 = lax.broadcasted_iota(jnp.int32, (128, 256), 0)
+    rows256 = lax.broadcasted_iota(jnp.int32, (256, 256), 0)
+    cols256 = lax.broadcasted_iota(jnp.int32, (256, 256), 1)
+    rows256w = lax.broadcasted_iota(jnp.int32, (256, wide), 0)
+    rows32 = lax.broadcasted_iota(jnp.int32, (32, wide), 0)
+    one_if = lambda m: jnp.where(m, F32(1), F32(0)).astype(BF16)
+    acc[...] = jnp.zeros_like(acc)
 
     def tile(kt, _):
         at = pl.ds(pl.multiple_of(kt * wide, wide), wide)
@@ -188,7 +196,6 @@
     for cp in ins:
         cp.start()
     kcopy = pltpu.make_async_copy(k_hbm, kmat, k_sem)
-    kcopy.start()
     barrier = pltpu.get_barrier_semaphore()
 
     gx_at = [lax.rem(gx + a, nx) for a in range(nx)]
@@ -220,8 +227,10 @@
     def arrive_blocks():
         for cp in ins[2:]:
             cp.wait()
+        kcopy.start()
+    rank_part(tgt_ref, slot_s, carry)
     stencil_part(fb_ref, pr_ref, loc_ref, w_ref, an_ref, trac, tab32, tab, idxt, wt, res, arrive_lists, arrive_blocks)
-    pack_part(tgt_ref, fn_ref, trac, slot_s, carry, acc_s, s_ref)
+    pack_part(tgt_ref, fn_ref, trac, slot_s, acc_s, s_ref)
     pl.semaphore_wait(barrier, n - 1)
 
     def near(src, dst, ss, rs, t):

time: 78.9 us -> 78.4 us (level)
  no operation moved by 1% of the time
where the time goes in v8:
time: 78.4 us; the launch traced here: 78.2 us
  Pallas kernels  76.4 us (97%)
  local copies, waits for them, and re-layouts  1.05 us (1%)
    pallas_call x1, Pallas kernels, solid(): pl.pallas_call(functools.partial(solid_kernel, nx, ny, shapes), out_shape...  73 us
    pallas_call x1, Pallas kernels, solid(): pl.pallas_call(functools.partial(unpack_kernel, n), out_shape=(jax.ShapeD...  3.43 us

profile of v8, /device:TPU:1, one launch (start us, length us, event | category | flops | bytes accessed | tf_op | source)
XLA Modules:
  0.0 78.2 jit_solution(7007969056643593503)
XLA Ops:
  0.6 0.0 copy-start.1
  0.6 73.0 %solid.1.ret_ref = f32[138,6,128]{2,1,0:T(8,128)} custom-call(s32[4096]{0:T(1024)} %fb_ref.1, bf16[256,4096]{1,0:T(8,128)(2,1)} %pr_hbm.1, s32[32,4096]{1,0:T(8,128)} %loc_hbm.1, f32[32,4096]{1,0:T(8,128)} %w_hbm.1, f32[12,4096]{1,0:T(8,128)} %an_hbm.1, s32[8,4096]{1,0:T(8,128)} %fn_hbm.1, s32[1,4096]{1,0:T(1,128)} %bitcast.2, f32[60,60,256]{2,1,0:T(8,128)} %k_hbm.1, ...), custom_call_target="tpu_custom_call" | custom-call | tf_op jit(solution)/shard_map/solid/pallas_call | solution.py:538
  73.7 0.0 copy-done.1
  73.7 0.0 copy-start
  73.7 1.0 %copy-done = f32[138,6,128]{2,1,0:T(8,128)S(1)} copy-done((f32[138,6,128]{2,1,0:T(8,128)S(1)}, f32[138,6,128]{2,1,0:T(8,128)}, u32[]{:S(2)}) %copy-start) | copy-done | bytes 423960
  74.7 3.4 %unpack.1 = (f32[3,1024]{1,0:T(4,128)}, f32[12,4096]{1,0:T(8,128)}) custom-call(s32[1,4096]{1,0:T(1,128)S(1)} %bitcast.3, f32[138,6,128]{2,1,0:T(8,128)S(1)} %copy-done), custom_call_target="tpu_custom_call" | custom-call | tf_op jit(solution)/shard_map/unpack/pallas_call | solution.py:559
Async XLA Ops:
  0.6 73.0 %copy-start.1 = (s32[4096,1]{0,1:T(1,128)S(1)}, s32[4096,1]{0,1:T(1,128)}, u32[]{:S(2)}) copy-start(s32[4096,1]{0,1:T(1,128)} %param.18) | copy-start | bytes 49156
  73.7 1.1 %copy-start = (f32[138,6,128]{2,1,0:T(8,128)S(1)}, f32[138,6,128]{2,1,0:T(8,128)}, u32[]{:S(2)}) copy-start(f32[138,6,128]{2,1,0:T(8,128)} %solid.1.ret_ref) | copy-start | bytes 1271812

commit v9 on v8

--- a/solution.py
+++ b/solution.py
@@ -160,7 +160,7 @@
         else:
             c, h = divmod(r - 32, 8)
             nd_ref[c:c + 1, 128 * h:128 * h + 128] = row
-    wide = 1024
+    wide = 2048
     rows128 = lax.broadcasted_iota(jnp.int32, (128, wide), 0)
     rows64 = lax.broadcasted_iota(jnp.int32, (64, wide), 0)
     for r in range(6):
@@ -177,7 +177,7 @@
             [jnp.sum(jnp.where(mask, y[64 * v:64 * v + 64, :], F32(0)), axis=0, keepdims=True) for v in range(12)], axis=0
         )
         return 0
-    lax.fori_loop(0, 4, tile, 0)
+    lax.fori_loop(0, 2, tile, 0)
 
 
 def solid_kernel(nx, ny, shapes, fb_ref, pr_hbm, loc_hbm, w_hbm, an_hbm, fn_hbm, tgt_ref, k_hbm, con_ref, halo_ref, mass_ref, disp_ref, vel_ref,

time: 78.4 us -> 78.2 us (level)
  no operation moved by 1% of the time
where the time goes in v9:
time: 78.2 us; the launch traced here: 78 us
  Pallas kernels  76.3 us (98%)
  local copies, waits for them, and re-layouts  1.05 us (1%)
    pallas_call x1, Pallas kernels, solid(): pl.pallas_call(functools.partial(solid_kernel, nx, ny, shapes), out_shape...  73 us
    pallas_call x1, Pallas kernels, solid(): pl.pallas_call(functools.partial(unpack_kernel, n), out_shape=(jax.ShapeD...  3.2 us

profile of v9, /device:TPU:1, one launch (start us, length us, event | category | flops | bytes accessed | tf_op | source)
XLA Modules:
  0.0 78.0 jit_solution(3711687224250714611)
XLA Ops:
  0.6 0.0 copy-start.1
  0.6 73.0 %solid.1.ret_ref = f32[138,6,128]{2,1,0:T(8,128)} custom-call(s32[4096]{0:T(1024)} %fb_ref.1, bf16[256,4096]{1,0:T(8,128)(2,1)} %pr_hbm.1, s32[32,4096]{1,0:T(8,128)} %loc_hbm.1, f32[32,4096]{1,0:T(8,128)} %w_hbm.1, f32[12,4096]{1,0:T(8,128)} %an_hbm.1, s32[8,4096]{1,0:T(8,128)} %fn_hbm.1, s32[1,4096]{1,0:T(1,128)} %bitcast.2, f32[60,60,256]{2,1,0:T(8,128)} %k_hbm.1, ...), custom_call_target="tpu_custom_call" | custom-call | tf_op jit(solution)/shard_map/solid/pallas_call | solution.py:538
  73.7 0.0 copy-done.1
  73.7 0.0 copy-start
  73.7 1.0 %copy-done = f32[138,6,128]{2,1,0:T(8,128)S(1)} copy-done((f32[138,6,128]{2,1,0:T(8,128)S(1)}, f32[138,6,128]{2,1,0:T(8,128)}, u32[]{:S(2)}) %copy-start) | copy-done | bytes 423960
  74.8 3.2 %unpack.1 = (f32[3,1024]{1,0:T(4,128)}, f32[12,4096]{1,0:T(8,128)}) custom-call(s32[1,4096]{1,0:T(1,128)S(1)} %bitcast.3, f32[138,6,128]{2,1,0:T(8,128)S(1)} %copy-done), custom_call_target="tpu_custom_call" | custom-call | tf_op jit(solution)/shard_map/unpack/pallas_call | solution.py:559
Async XLA Ops:
  0.6 73.1 %copy-start.1 = (s32[4096,1]{0,1:T(1,128)S(1)}, s32[4096,1]{0,1:T(1,128)}, u32[]{:S(2)}) copy-start(s32[4096,1]{0,1:T(1,128)} %param.18) | copy-start | bytes 49156
  73.7 1.1 %copy-start = (f32[138,6,128]{2,1,0:T(8,128)S(1)}, f32[138,6,128]{2,1,0:T(8,128)}, u32[]{:S(2)}) copy-start(f32[138,6,128]{2,1,0:T(8,128)} %solid.1.ret_ref) | copy-start | bytes 1271812
